TPU v7x, 32 devices: a whole 2x2x4 slice. The times are simulated.
32 devices in a mesh: ty: 8 (over y, x, core), tx: 4 (over z).
Axes of the slice: x: 2, y: 2, z: 4, core: 2. Of those that a mesh axis runs over, the one named last changes fastest.
Arguments:
- noise: float32 [1024, 1024], P('ty', 'tx'), may hold values from -6 to 6
- root_spectrum: float32 [384, 512], replicated, may hold values from 0.25 to 4
Outputs:
- field: float32 [1024, 1024], P('ty', 'tx')
All inputs are finite; a program needn't handle non-finite values.
Results may differ from a plain program's by a relative error of at most 0.0003.
Values sent between devices are 32-bit elements; how exact they have to be, the bound alone decides.
No kernel may reach another device: no remote copies, remote signals or barrier semaphores. Data moves between devices by JAX's collectives and lax.ppermute only.
A program may use at most 64 MiB of HBM per device.

v0:
```python
import functools
import math

import numpy as np
import jax
import jax.numpy as jnp
from jax import lax
from jax.experimental import pallas as pl
from jax.experimental.pallas import tpu as pltpu
from jax.sharding import PartitionSpec as P

F32 = jnp.float32
BF16 = jnp.bfloat16


def halves(table):
    high = table.astype(BF16)
    low = (table - high.astype(np.float64)).astype(BF16)
    return [high, low]


def row_tables(cols):
    half = cols // 2
    quarter = cols // 4
    c = np.arange(half)[:, None]
    m = np.arange(quarter)[None, :]
    sign = (1.0 - 2.0 * (np.arange(half) % 2))
    even = 2.0 * np.pi * ((2 * m * c) % cols) / cols
    odd = 2.0 * np.pi * (((2 * m + 1) * c) % cols) / cols
    even_sine = -np.sin(even)
    even_sine[:, 0] = sign
    forward_even = np.concatenate([np.cos(even), even_sine], axis=1)
    forward_odd = np.concatenate([np.cos(odd), -np.sin(odd)], axis=1)
    twice = np.full((half, 1), 2.0)
    twice[0] = 1.0
    twice[quarter] = 1.0
    back_even = forward_even.T * twice
    back_odd = forward_odd.T * 2.0
    return np.stack(halves(forward_even) + halves(forward_odd) + halves(back_even) + halves(back_odd))


def column_tables(rows):
    third = rows // 3
    q = np.arange(third)[:, None]
    s = np.arange(third)[None, :]
    forward = []
    back = []
    for p in range(3):
        angle = 2.0 * np.pi * (((3 * q + p) * s) % rows) / rows
        table = np.block([[np.cos(angle), np.sin(angle)], [-np.sin(angle), np.cos(angle)]])
        forward += halves(table)
        back += halves(table.T)
    return np.stack(forward), np.stack(back)


def mirror_tables(rows):
    third = rows // 3
    eye = np.eye(third)
    zero = np.zeros((third, third))
    same = eye[(-np.arange(third)) % third]
    swapped = eye[::-1]
    return np.stack([np.block([[m, zero], [zero, -m]]) for m in (same, swapped)]).astype(BF16)


def split(values):
    high = values.astype(BF16)
    return high, (values - high.astype(F32)).astype(BF16)


def dot(left, right):
    return jnp.dot(left, right, preferred_element_type=F32)


def by_table(values, high, low):
    first, second = split(values)
    return dot(first, high) + dot(second, high) + dot(first, low)


def from_table(high, low, values):
    first, second = split(values)
    return dot(high, first) + dot(high, second) + dot(low, first)


def spectrum_kernel(root_ref, mixed_ref, crossed_ref):
    rows, cols = root_ref.shape
    third = rows // 3
    half = cols // 2
    quarter = cols // 4
    root = root_ref[...]
    k = lax.broadcasted_iota(jnp.int32, (cols, half), 0)
    lane = lax.broadcasted_iota(jnp.int32, (cols, half), 1)
    wanted = jnp.where(lane < quarter, 2 * lane, 2 * (lane - quarter) + 1)
    mirrored = jnp.where(wanted == 0, 0, cols - wanted)
    first_lane = lane == 0
    share = jnp.where(first_lane, 0.5, 1.0)
    nyquist = jnp.logical_and(first_lane, k == half)
    pick = jnp.where(jnp.logical_or(k == wanted, nyquist), share, 0.0).astype(BF16)
    pick_mirrored = jnp.where(jnp.logical_or(k == mirrored, nyquist), share, 0.0).astype(BF16)
    high, low = split(root)
    chosen = dot(high, pick) + dot(low, pick)
    chosen_mirrored = dot(high, pick_mirrored) + dot(low, pick_mirrored)
    difference = 0.5 * (root[:, :quarter] - root[:, half:half + quarter])
    i = lax.broadcasted_iota(jnp.int32, (third, rows), 0)
    j = lax.broadcasted_iota(jnp.int32, (third, rows), 1)
    scale = 0.5 / (rows * cols)
    c_high, c_low = split(chosen)
    m_high, m_low = split(chosen_mirrored)
    d_high, d_low = split(difference)
    block_lane = lax.broadcasted_iota(jnp.int32, (third, quarter), 1)
    for p in range(3):
        source = 3 * i + p
        target = rows - source
        target = jnp.where(target == rows, 0, target)
        order = jnp.where(j == source, 1.0, 0.0).astype(BF16)
        order_mirrored = jnp.where(j == target, 1.0, 0.0).astype(BF16)
        both = jnp.where(j == source, 1.0, 0.0) + jnp.where(j == target, 1.0, 0.0)
        both = both.astype(BF16)
        mixed = dot(order, c_high) + dot(order, c_low) + dot(order_mirrored, m_high) + dot(order_mirrored, m_low)
        mixed_ref[p * third:(p + 1) * third, :] = mixed * scale
        crossed = dot(both, d_high) + dot(both, d_low)
        crossed_ref[p * third:(p + 1) * third, :] = jnp.where(block_lane == 0, crossed * scale, 0.0)


def filter_kernel(mid_0, mid_1, mid_2, side_0, side_1, side_2, mixed_ref, crossed_ref, row_ref, forward_ref, back_ref,
                  mirror_ref, mid_out_0, mid_out_1, mid_out_2, side_out_0, side_out_1, side_out_2, real_ref, imag_ref,
                  spec_ref):
    third = mid_0.shape[0]
    half = mid_0.shape[1]
    quarter = half // 2
    root_three = math.sqrt(3.0) / 2.0
    for j, (mid, side) in enumerate(((mid_0, side_0), (mid_1, side_1), (mid_2, side_2))):
        left = side[:, :quarter]
        right = side[:, quarter:]
        first = mid[:, :quarter]
        second = mid[:, quarter:]
        even = jnp.concatenate([left + second, first + right], axis=1)
        odd = jnp.concatenate([left - second, first - right], axis=1)
        even = by_table(even, row_ref[0], row_ref[1])
        odd = by_table(odd, row_ref[2], row_ref[3])
        real_ref[j, :, :quarter] = even[:, :quarter]
        real_ref[j, :, quarter:] = odd[:, :quarter]
        imag_ref[j, :, :quarter] = even[:, quarter:]
        imag_ref[j, :, quarter:] = odd[:, quarter:]
    sum_real = real_ref[1] + real_ref[2]
    sum_imag = imag_ref[1] + imag_ref[2]
    gap_real = root_three * (real_ref[1] - real_ref[2])
    gap_imag = root_three * (imag_ref[1] - imag_ref[2])
    base_real = real_ref[0] - 0.5 * sum_real
    base_imag = imag_ref[0] - 0.5 * sum_imag
    inputs = (
        (real_ref[0] + sum_real, imag_ref[0] + sum_imag),
        (base_real + gap_imag, base_imag - gap_real),
        (base_real - gap_imag, base_imag + gap_real),
    )
    for p, pair in enumerate(inputs):
        stacked = jnp.concatenate(pair, axis=0)
        spec_ref[p] = from_table(forward_ref[2 * p], forward_ref[2 * p + 1], stacked)
    packed = []
    for p in range(3):
        high, low = split(spec_ref[(3 - p) % 3, :, :quarter])
        flipped = dot(mirror_ref[min(p, 1)], jnp.concatenate([high, low], axis=1))
        packed.append(flipped[:, :quarter] + flipped[:, quarter:])
    outs = []
    for p in range(3):
        mixed = mixed_ref[p * third:(p + 1) * third, :]
        mixed = jnp.concatenate([mixed, mixed], axis=0)
        crossed = crossed_ref[p * third:(p + 1) * third, :]
        crossed = jnp.concatenate([crossed, crossed], axis=0)
        filtered = spec_ref[p] * mixed
        filtered = jnp.concatenate([filtered[:, :quarter] + packed[p] * crossed, filtered[:, quarter:]], axis=1)
        outs.append(from_table(back_ref[2 * p], back_ref[2 * p + 1], filtered))
    real = [value[:third] for value in outs]
    imag = [value[third:] for value in outs]
    sum_real = real[1] + real[2]
    sum_imag = imag[1] + imag[2]
    gap_real = root_three * (real[1] - real[2])
    gap_imag = root_three * (imag[1] - imag[2])
    base_real = real[0] - 0.5 * sum_real
    base_imag = imag[0] - 0.5 * sum_imag
    blocks = (
        (real[0] + sum_real, imag[0] + sum_imag),
        (base_real - gap_imag, base_imag + gap_real),
        (base_real + gap_imag, base_imag - gap_real),
    )
    lane = lax.broadcasted_iota(jnp.int32, (1, half), 1).astype(F32)
    rising = (lane + 0.5) / half
    falling = 1.0 - rising
    row = lax.broadcasted_iota(jnp.int32, (third, 1), 0).astype(F32)
    for j, (block, mid_out, side_out) in enumerate(
        zip(blocks, (mid_out_0, mid_out_1, mid_out_2), (side_out_0, side_out_1, side_out_2))
    ):
        knots = (row + 0.5) / third + j
        if j == 0:
            weight = 0.5 * knots * knots
        elif j == 1:
            weight = 0.5 * (-2.0 * knots * knots + 6.0 * knots - 3.0)
        else:
            weight = 0.5 * (3.0 - knots) * (3.0 - knots)
        even = jnp.concatenate([block[0][:, :quarter], block[1][:, :quarter]], axis=1)
        odd = jnp.concatenate([block[0][:, quarter:], block[1][:, quarter:]], axis=1)
        even = by_table(even, row_ref[4], row_ref[5])
        odd = by_table(odd, row_ref[6], row_ref[7])
        lower = (even + odd) * (weight * rising)
        upper = (even - odd) * (weight * falling)
        side_out[:, :quarter] = lower[:, :quarter]
        side_out[:, quarter:] = upper[:, quarter:]
        mid_out[:, :quarter] = lower[:, quarter:]
        mid_out[:, quarter:] = upper[:, :quarter]


def whole(count):
    return [pl.BlockSpec(memory_space=pltpu.VMEM)] * count


def passed_along(shard, axis, by):
    length = lax.axis_size(axis)
    return lax.ppermute(shard, axis, [(i, (i + by) % length) for i in range(length)])


def per_device(noise, root_spectrum):
    margin, block_cols = noise.shape
    rows, cols = root_spectrum.shape
    row_table = jnp.asarray(row_tables(cols))
    forward_table, back_table = (jnp.asarray(t) for t in column_tables(rows))
    mirror_table = jnp.asarray(mirror_tables(rows))
    limit = pltpu.CompilerParams(vmem_limit_bytes=24 * 1024 * 1024)
    mixed, crossed = pl.pallas_call(
        spectrum_kernel,
        out_shape=(jax.ShapeDtypeStruct((rows, cols // 2), F32), jax.ShapeDtypeStruct((rows, cols // 4), F32)),
        in_specs=whole(1),
        out_specs=tuple(whole(2)),
        compiler_params=limit,
        cost_estimate=pl.CostEstimate(flops=2 * 10**9, bytes_accessed=10**6, transcendentals=0),
        name="spectrum",
    )(root_spectrum)
    from_left = passed_along(noise[:, block_cols - margin:], "tx", 1)
    from_right = passed_along(noise[:, :margin], "tx", -1)
    upper = passed_along(noise, "ty", 1)
    lower = passed_along(noise, "ty", -1)
    side = jnp.concatenate([from_left, from_right], axis=1)
    upper_side = passed_along(side, "ty", 1)
    lower_side = passed_along(side, "ty", -1)
    block = jax.ShapeDtypeStruct((margin, block_cols), F32)
    mid_0, mid_1, mid_2, side_0, side_1, side_2 = pl.pallas_call(
        filter_kernel,
        out_shape=(block,) * 6,
        in_specs=whole(12),
        out_specs=tuple(whole(6)),
        scratch_shapes=[
            pltpu.VMEM((3, margin, block_cols), F32),
            pltpu.VMEM((3, margin, block_cols), F32),
            pltpu.VMEM((3, 2 * margin, block_cols), F32),
        ],
        compiler_params=limit,
        cost_estimate=pl.CostEstimate(flops=4 * 10**9, bytes_accessed=10**7, transcendentals=0),
        name="filter",
    )(upper, noise, lower, upper_side, side, lower_side, mixed, crossed, row_table, forward_table, back_table,
      mirror_table)
    side = side_1 + passed_along(side_0, "ty", -1) + passed_along(side_2, "ty", 1)
    to_right = passed_along(side[:, margin:], "tx", 1)
    to_left = passed_along(side[:, :margin], "tx", -1)
    mid = mid_1 + passed_along(mid_0, "ty", -1) + passed_along(mid_2, "ty", 1)
    return mid + jnp.concatenate([to_right, to_left], axis=1)


def solution(mesh):
    placed = (P("ty", "tx"), P())
    return jax.shard_map(
        per_device, mesh=mesh, in_specs=placed, out_specs=P("ty", "tx"), check_vma=False
    )
```

profile of v0, /device:TPU:0, one launch (start us, length us, event | category | flops | bytes accessed | tf_op | source)
XLA Modules:
  0.0 33.6 jit_solution(10257214962523879463)
XLA Ops:
  0.0 0.9 %fusion.1 = (f32[128,128]{1,0:T(8,128)S(1)}, f32[128,128]{1,0:T(8,128)S(1)}) fusion(f32[128,256]{1,0:T(8,128)} %mid_1.1), kind=kLoop, calls=%fused_computation.5 | loop fusion | bytes 262144 | tf_op jit(solution)/shard_map/slice | solution.py:237
  0.9 3.1 %collective-permute-start.2 = (f32[128,128]{1,0:T(8,128)S(1)}, f32[128,128]{1,0:T(8,128)S(1)}, u32[]{:S(2)}, u32[]{:S(2)}) collective-permute-start(f32[128,128]{1,0:T(8,128)S(1)} %get-tuple-element.24), channel_id=1, source_target_pairs={{0,1},{1,2},{2,3},{3,0},{4,5},{5,6},{6,7},{7,4},{8,9},{9,10},{10,1... | collective-permute-start | bytes 196616 | tf_op jit(solution)/shard_map/ppermute | solution.py:217
  4.0 1.6 %collective-permute-start.1 = (f32[128,256]{1,0:T(8,128)S(1)}, f32[128,256]{1,0:T(8,128)S(1)}, u32[]{:S(2)}, u32[]{:S(2)}) collective-permute-start(f32[128,256]{1,0:T(8,128)S(1)} %copy-done), channel_id=1, source_target_pairs={{0,28},{4,0},{8,4},{12,8},{16,12},{20,16},{24,20},{28,24},{1,29},{... | collective-permute-start | bytes 393224 | tf_op jit(solution)/shard_map/ppermute | solution.py:217
  5.6 0.0 collective-permute-start
  5.6 2.4 %collective-permute-start.3 = (f32[128,128]{1,0:T(8,128)S(1)}, f32[128,128]{1,0:T(8,128)S(1)}, u32[]{:S(2)}, u32[]{:S(2)}) collective-permute-start(f32[128,128]{1,0:T(8,128)S(1)} %get-tuple-element.23), channel_id=1, source_target_pairs={{0,3},{1,0},{2,1},{3,2},{4,7},{5,4},{6,5},{7,6},{8,11},{9,8},{10,9... | collective-permute-start | bytes 196616 | tf_op jit(solution)/shard_map/ppermute | solution.py:217
  8.0 0.3 collective-permute-done.2
  8.3 1.6 %collective-permute-done.3 = f32[128,128]{1,0:T(8,128)S(1)} collective-permute-done((f32[128,128]{1,0:T(8,128)S(1)}, f32[128,128]{1,0:T(8,128)S(1)}, u32[]{:S(2)}, u32[]{:S(2)}) %collective-permute-start.3) | collective-permute-done | bytes 65568 | tf_op jit(solution)/shard_map/ppermute | solution.py:217
  9.9 1.9 %collective-permute-start.5 = (f32[128,256]{1,0:T(8,128)S(1)}, f32[128,256]{1,0:T(8,128)S(1)}, u32[]{:S(2)}, u32[]{:S(2)}) collective-permute-start(f32[128,256]{1,0:T(8,128)S(1)} %constant_dynamic-update-slice_fusion.side_1), channel_id=1, source_target_pairs={{0,28},{4,0},{8,4},{12,8},{16,12},{20,16},{24,20},{28,24},{1,29},{... | collective-permute-start | bytes 393224 | tf_op jit(solution)/shard_map/ppermute | solution.py:217
  11.8 0.0 collective-permute-start.4
  11.8 1.1 %copy-done.1 = f32[384,512]{1,0:T(8,128)S(1)} copy-done((f32[384,512]{1,0:T(8,128)S(1)}, f32[384,512]{1,0:T(8,128)}, u32[]{:S(2)}) %copy-start.1) | copy-done | bytes 786456
  13.0 1.4 %spectrum.1 = (f32[384,256]{1,0:T(8,128)S(1)}, f32[384,128]{1,0:T(8,128)S(1)}) custom-call(f32[384,512]{1,0:T(8,128)S(1)} %copy-done.1), custom_call_target="tpu_custom_call" | custom-call | flops 2000000000 | bytes 1000000 | tf_op jit(solution)/shard_map/spectrum/pallas_call | solution.py:227
  14.4 0.1 collective-permute-done.5.side_2
  14.5 2.6 %collective-permute-done.4.side_0 = f32[128,256]{1,0:T(8,128)S(1)} collective-permute-done((f32[128,256]{1,0:T(8,128)S(1)}, f32[128,256]{1,0:T(8,128)S(1)}, u32[]{:S(2)}, u32[]{:S(2)}) %collective-permute-start.4) | collective-permute-done | bytes 131104 | tf_op jit(solution)/shard_map/ppermute | solution.py:217
  17.1 2.3 %filter.1 = (f32[128,256]{1,0:T(8,128)S(1)}, f32[128,256]{1,0:T(8,128)S(1)}, f32[128,256]{1,0:T(8,128)S(1)}, f32[128,256]{1,0:T(8,128)S(1)}, f32[128,256]{1,0:T(8,128)S(1)}, /*index=5*/f32[128,256]{1,0:T(8,128)S(1)}) custom-call(f32[128,256]{1,0:T(8,128)S(1)} %collective-permute-done.mid_0, f32[128,256]{1,0:T(8,128)S(1)} %copy-done, ...), custom_call_target="tpu_custom_call" | custom-call | flops 4000000000 | bytes 10000000 | tf_op jit(solution)/shard_map/filter/pallas_call | solution.py:244
  19.4 0.3 collective-permute-start.8
  19.7 0.3 collective-permute-start.9
  20.0 2.3 %collective-permute-start.6 = (f32[128,256]{1,0:T(8,128)S(1)}, f32[128,256]{1,0:T(8,128)S(1)}, u32[]{:S(2)}, u32[]{:S(2)}) collective-permute-start(f32[128,256]{1,0:T(8,128)S(1)} %get-tuple-element.16), channel_id=1, source_target_pairs={{0,28},{4,0},{8,4},{12,8},{16,12},{20,16},{24,20},{28,24},{1,29},{... | collective-permute-start | bytes 393224 | tf_op jit(solution)/shard_map/ppermute | solution.py:217
  22.3 1.2 %collective-permute-done.8 = f32[128,256]{1,0:T(8,128)S(1)} collective-permute-done((f32[128,256]{1,0:T(8,128)S(1)}, f32[128,256]{1,0:T(8,128)S(1)}, u32[]{:S(2)}, u32[]{:S(2)}) %collective-permute-start.8) | collective-permute-done | bytes 131104 | tf_op jit(solution)/shard_map/ppermute | solution.py:217
  23.6 2.5 %collective-permute-done.9 = f32[128,256]{1,0:T(8,128)S(1)} collective-permute-done((f32[128,256]{1,0:T(8,128)S(1)}, f32[128,256]{1,0:T(8,128)S(1)}, u32[]{:S(2)}, u32[]{:S(2)}) %collective-permute-start.9) | collective-permute-done | bytes 131104 | tf_op jit(solution)/shard_map/ppermute | solution.py:217
  26.1 1.8 %collective-permute-start.10 = (f32[128,128]{1,0:T(8,128)S(1)}, f32[128,128]{1,0:T(8,128)S(1)}, u32[]{:S(2)}, u32[]{:S(2)}) collective-permute-start(f32[128,128]{1,0:T(8,128)S(1)} %get-tuple-element.21), channel_id=1, source_target_pairs={{0,1},{1,2},{2,3},{3,0},{4,5},{5,6},{6,7},{7,4},{8,9},{9,10},{10,1... | collective-permute-start | bytes 196616 | tf_op jit(solution)/shard_map/ppermute | solution.py:217
  27.9 2.1 %collective-permute-start.11 = (f32[128,128]{1,0:T(8,128)S(1)}, f32[128,128]{1,0:T(8,128)S(1)}, u32[]{:S(2)}, u32[]{:S(2)}) collective-permute-start(f32[128,128]{1,0:T(8,128)S(1)} %get-tuple-element.22), channel_id=1, source_target_pairs={{0,3},{1,0},{2,1},{3,2},{4,7},{5,4},{6,5},{7,6},{8,11},{9,8},{10,9... | collective-permute-start | bytes 196616 | tf_op jit(solution)/shard_map/ppermute | solution.py:217
  30.0 2.3 %collective-permute-done.10 = f32[128,128]{1,0:T(8,128)S(1)} collective-permute-done((f32[128,128]{1,0:T(8,128)S(1)}, f32[128,128]{1,0:T(8,128)S(1)}, u32[]{:S(2)}, u32[]{:S(2)}) %collective-permute-start.10) | collective-permute-done | bytes 65568 | tf_op jit(solution)/shard_map/ppermute | solution.py:217
  32.4 0.5 %collective-permute-done.11 = f32[128,128]{1,0:T(8,128)S(1)} collective-permute-done((f32[128,128]{1,0:T(8,128)S(1)}, f32[128,128]{1,0:T(8,128)S(1)}, u32[]{:S(2)}, u32[]{:S(2)}) %collective-permute-start.11) | collective-permute-done | bytes 65568 | tf_op jit(solution)/shard_map/ppermute | solution.py:217
  32.9 0.7 %maximum_add_fusion = f32[128,256]{1,0:T(8,128)} fusion(f32[128,128]{1,0:T(8,128)S(1)} %collective-permute-done.11, f32[128,128]{1,0:T(8,128)S(1)} %collective-permute-done.10, f32[128,256]{1,0:T(8,128)S(1)} %collective-permute-done.7, f32[128,256]{1,0:T(8,128)S(1)} %get-tuple-element.15, f32[128,256]{1,0:T(8,128)S(1)} %collective-permute-done.6), kind=kLoop, calls=%fused_computation | loop fusion | flops 131072 | bytes 655360 | tf_op jit(solution)/shard_map/add | solution.py:263
  (20 shorter events, 0.1 us)
Async XLA Ops:
  0.0 4.0 %copy-start = (f32[128,256]{1,0:T(8,128)S(1)}, f32[128,256]{1,0:T(8,128)}, u32[]{:S(2)}) copy-start(f32[128,256]{1,0:T(8,128)} %mid_1.1) | copy-start | bytes 393220
  0.9 7.4 %collective-permute-start.2 = (f32[128,128]{1,0:T(8,128)S(1)}, f32[128,128]{1,0:T(8,128)S(1)}, u32[]{:S(2)}, u32[]{:S(2)}) collective-permute-start(f32[128,128]{1,0:T(8,128)S(1)} %get-tuple-element.24), channel_id=1, source_target_pairs={{0,1},{1,2},{2,3},{3,0},{4,5},{5,6},{6,7},{7,4},{8,9},{9,10},{10,1... | collective-permute-start | bytes 196616 | tf_op jit(solution)/shard_map/ppermute | solution.py:217
  4.0 10.3 %collective-permute-start.1 = (f32[128,256]{1,0:T(8,128)S(1)}, f32[128,256]{1,0:T(8,128)S(1)}, u32[]{:S(2)}, u32[]{:S(2)}) collective-permute-start(f32[128,256]{1,0:T(8,128)S(1)} %copy-done), channel_id=1, source_target_pairs={{0,28},{4,0},{8,4},{12,8},{16,12},{20,16},{24,20},{28,24},{1,29},{... | collective-permute-start | bytes 393224 | tf_op jit(solution)/shard_map/ppermute | solution.py:217
  5.6 8.7 %collective-permute-start = (f32[128,256]{1,0:T(8,128)S(1)}, f32[128,256]{1,0:T(8,128)S(1)}, u32[]{:S(2)}, u32[]{:S(2)}) collective-permute-start(f32[128,256]{1,0:T(8,128)S(1)} %copy-done), channel_id=1, source_target_pairs={{0,4},{4,8},{8,12},{12,16},{16,20},{20,24},{24,28},{28,0},{1,5},{5... | collective-permute-start | bytes 393224 | tf_op jit(solution)/shard_map/ppermute | solution.py:217
  5.6 4.3 %collective-permute-start.3 = (f32[128,128]{1,0:T(8,128)S(1)}, f32[128,128]{1,0:T(8,128)S(1)}, u32[]{:S(2)}, u32[]{:S(2)}) collective-permute-start(f32[128,128]{1,0:T(8,128)S(1)} %get-tuple-element.23), channel_id=1, source_target_pairs={{0,3},{1,0},{2,1},{3,2},{4,7},{5,4},{6,5},{7,6},{8,11},{9,8},{10,9... | collective-permute-start | bytes 196616 | tf_op jit(solution)/shard_map/ppermute | solution.py:217
  9.9 4.5 %collective-permute-start.5 = (f32[128,256]{1,0:T(8,128)S(1)}, f32[128,256]{1,0:T(8,128)S(1)}, u32[]{:S(2)}, u32[]{:S(2)}) collective-permute-start(f32[128,256]{1,0:T(8,128)S(1)} %constant_dynamic-update-slice_fusion.side_1), channel_id=1, source_target_pairs={{0,28},{4,0},{8,4},{12,8},{16,12},{20,16},{24,20},{28,24},{1,29},{... | collective-permute-start | bytes 393224 | tf_op jit(solution)/shard_map/ppermute | solution.py:217
  11.8 5.3 %collective-permute-start.4 = (f32[128,256]{1,0:T(8,128)S(1)}, f32[128,256]{1,0:T(8,128)S(1)}, u32[]{:S(2)}, u32[]{:S(2)}) collective-permute-start(f32[128,256]{1,0:T(8,128)S(1)} %constant_dynamic-update-slice_fusion.side_1), channel_id=1, source_target_pairs={{0,4},{4,8},{8,12},{12,16},{16,20},{20,24},{24,28},{28,0},{1,5},{5... | collective-permute-start | bytes 393224 | tf_op jit(solution)/shard_map/ppermute | solution.py:217
  11.8 1.1 %copy-start.1 = (f32[384,512]{1,0:T(8,128)S(1)}, f32[384,512]{1,0:T(8,128)}, u32[]{:S(2)}) copy-start(f32[384,512]{1,0:T(8,128)} %root_ref.1) | copy-start | bytes 2359300
  12.9 4.2 %copy-start.2 = (bf16[8,256,256]{2,1,0:T(8,128)(2,1)S(1)}, bf16[8,256,256]{2,1,0:T(8,128)(2,1)}, u32[]{:S(2)}) copy-start(bf16[8,256,256]{2,1,0:T(8,128)(2,1)} %constant.8.clone.row_ref) | copy-start | bytes 3145732
  12.9 4.2 %copy-start.3 = (bf16[6,256,256]{2,1,0:T(8,128)(2,1)S(1)}, bf16[6,256,256]{2,1,0:T(8,128)(2,1)}, u32[]{:S(2)}) copy-start(bf16[6,256,256]{2,1,0:T(8,128)(2,1)} %constant.10.clone.back_ref) | copy-start | bytes 2359300
  12.9 4.2 %copy-start.4 = (bf16[6,256,256]{2,1,0:T(8,128)(2,1)S(1)}, bf16[6,256,256]{2,1,0:T(8,128)(2,1)}, u32[]{:S(2)}) copy-start(bf16[6,256,256]{2,1,0:T(8,128)(2,1)} %constant.9.clone.forward_ref) | copy-start | bytes 2359300
  12.9 4.2 %copy-start.5 = (bf16[2,256,256]{2,1,0:T(8,128)(2,1)S(1)}, bf16[2,256,256]{2,1,0:T(8,128)(2,1)}, u32[]{:S(2)}) copy-start(bf16[2,256,256]{2,1,0:T(8,128)(2,1)} %constant.11.clone.mirror_ref) | copy-start | bytes 786436
  19.4 4.1 %collective-permute-start.8 = (f32[128,256]{1,0:T(8,128)S(1)}, f32[128,256]{1,0:T(8,128)S(1)}, u32[]{:S(2)}, u32[]{:S(2)}) collective-permute-start(f32[128,256]{1,0:T(8,128)S(1)} %get-tuple-element.19), channel_id=1, source_target_pairs={{0,28},{4,0},{8,4},{12,8},{16,12},{20,16},{24,20},{28,24},{1,29},{... | collective-permute-start | bytes 393224 | tf_op jit(solution)/shard_map/ppermute | solution.py:217
  19.7 6.4 %collective-permute-start.9 = (f32[128,256]{1,0:T(8,128)S(1)}, f32[128,256]{1,0:T(8,128)S(1)}, u32[]{:S(2)}, u32[]{:S(2)}) collective-permute-start(f32[128,256]{1,0:T(8,128)S(1)} %get-tuple-element.20), channel_id=1, source_target_pairs={{0,4},{4,8},{8,12},{12,16},{16,20},{20,24},{24,28},{28,0},{1,5},{5... | collective-permute-start | bytes 393224 | tf_op jit(solution)/shard_map/ppermute | solution.py:217
  20.0 10.1 %collective-permute-start.6 = (f32[128,256]{1,0:T(8,128)S(1)}, f32[128,256]{1,0:T(8,128)S(1)}, u32[]{:S(2)}, u32[]{:S(2)}) collective-permute-start(f32[128,256]{1,0:T(8,128)S(1)} %get-tuple-element.16), channel_id=1, source_target_pairs={{0,28},{4,0},{8,4},{12,8},{16,12},{20,16},{24,20},{28,24},{1,29},{... | collective-permute-start | bytes 393224 | tf_op jit(solution)/shard_map/ppermute | solution.py:217
  22.3 7.7 %collective-permute-start.7 = (f32[128,256]{1,0:T(8,128)S(1)}, f32[128,256]{1,0:T(8,128)S(1)}, u32[]{:S(2)}, u32[]{:S(2)}) collective-permute-start(f32[128,256]{1,0:T(8,128)S(1)} %get-tuple-element.17), channel_id=1, source_target_pairs={{0,4},{4,8},{8,12},{12,16},{16,20},{20,24},{24,28},{28,0},{1,5},{5... | collective-permute-start | bytes 393224 | tf_op jit(solution)/shard_map/ppermute | solution.py:217
  26.1 6.2 %collective-permute-start.10 = (f32[128,128]{1,0:T(8,128)S(1)}, f32[128,128]{1,0:T(8,128)S(1)}, u32[]{:S(2)}, u32[]{:S(2)}) collective-permute-start(f32[128,128]{1,0:T(8,128)S(1)} %get-tuple-element.21), channel_id=1, source_target_pairs={{0,1},{1,2},{2,3},{3,0},{4,5},{5,6},{6,7},{7,4},{8,9},{9,10},{10,1... | collective-permute-start | bytes 196616 | tf_op jit(solution)/shard_map/ppermute | solution.py:217
  27.9 5.0 %collective-permute-start.11 = (f32[128,128]{1,0:T(8,128)S(1)}, f32[128,128]{1,0:T(8,128)S(1)}, u32[]{:S(2)}, u32[]{:S(2)}) collective-permute-start(f32[128,128]{1,0:T(8,128)S(1)} %get-tuple-element.22), channel_id=1, source_target_pairs={{0,3},{1,0},{2,1},{3,2},{4,7},{5,4},{6,5},{7,6},{8,11},{9,8},{10,9... | collective-permute-start | bytes 196616 | tf_op jit(solution)/shard_map/ppermute | solution.py:217
where the time goes:
time: 33.7 us; the launch traced here: 33.6 us
  starting transfers between devices  15.8 us (47%)
  waiting for transfers between devices  11.2 us (33%)
  Pallas kernels  3.71 us (11%)
  local copies, waits for them, and re-layouts  2.1 us (6%)
  other arithmetic  0.71 us (2%)
    ppermute x12, starting transfers between devices, passed_along(): lax.ppermute(shard, axis, [(i, (i + by) % length) for i in range(length)])  15.8 us
    ppermute x12, waiting for transfers between devices, passed_along(): lax.ppermute(shard, axis, [(i, (i + by) % length) for i in range(length)])  11.2 us
    pallas_call x1, Pallas kernels, per_device(): pl.pallas_call(filter_kernel, out_shape=(block,) * 6, in_specs=whole(12),...  2.29 us
    pallas_call x1, Pallas kernels, per_device(): pl.pallas_call(spectrum_kernel, out_shape=(jax.ShapeDtypeStruct((rows, co...  1.41 us
    unnamed x13, local copies, waits for them, and re-layouts  1.16 us
    slice x1, local copies, waits for them, and re-layouts, per_device(): from_right = passed_along(noise[:, :margin], 'tx', -1)  0.92 us
    add x1, other arithmetic, per_device(): return mid + jnp.concatenate([to_right, to_left], axis=1)  0.69 us
  transfers between devices with their start and end apart: 12, of which 8 were waited for; matrix products, arithmetic and copies ran while one was open for 0% of the time, Pallas kernels for 4%

commit v1 on v0

--- a/solution.py
+++ b/solution.py
@@ -1,4 +1,3 @@
-import functools
 import math
 
 import numpy as np
@@ -8,6 +7,7 @@
 from jax.experimental import pallas as pl
 from jax.experimental.pallas import tpu as pltpu
 from jax.sharding import PartitionSpec as P
+
 
 F32 = jnp.float32
 BF16 = jnp.bfloat16
@@ -121,16 +121,25 @@
         crossed_ref[p * third:(p + 1) * third, :] = jnp.where(block_lane == 0, crossed * scale, 0.0)
 
 
-def filter_kernel(mid_0, mid_1, mid_2, side_0, side_1, side_2, mixed_ref, crossed_ref, row_ref, forward_ref, back_ref,
-                  mirror_ref, mid_out_0, mid_out_1, mid_out_2, side_out_0, side_out_1, side_out_2, real_ref, imag_ref,
+def swapped(odd, first, second):
+    return jnp.where(odd, second, first), jnp.where(odd, first, second)
+
+
+def filter_kernel(mid_far, mid_own, mid_near, far_far, far_own, far_near, near_far, near_own, near_near, mixed_ref,
+                  crossed_ref, row_ref, forward_ref, back_ref, mirror_ref, mid_far_out, mid_own_out, mid_near_out,
+                  far_far_out, far_own_out, far_near_out, near_far_out, near_own_out, near_near_out, real_ref, imag_ref,
                   spec_ref):
-    third = mid_0.shape[0]
-    half = mid_0.shape[1]
+    third, half = mid_own.shape
     quarter = half // 2
     root_three = math.sqrt(3.0) / 2.0
-    for j, (mid, side) in enumerate(((mid_0, side_0), (mid_1, side_1), (mid_2, side_2))):
-        left = side[:, :quarter]
-        right = side[:, quarter:]
+    odd_row = lax.axis_index("ty") % 2 == 1
+    odd_col = lax.axis_index("tx") % 2 == 1
+    mid_0, mid_2 = swapped(odd_row, mid_far[...], mid_near[...])
+    far_0, far_2 = swapped(odd_row, far_far[...], far_near[...])
+    near_0, near_2 = swapped(odd_row, near_far[...], near_near[...])
+    parts = ((mid_0, far_0, near_0), (mid_own[...], far_own[...], near_own[...]), (mid_2, far_2, near_2))
+    for j, (mid, far, near) in enumerate(parts):
+        left, right = swapped(odd_col, far, near)
         first = mid[:, :quarter]
         second = mid[:, quarter:]
         even = jnp.concatenate([left + second, first + right], axis=1)
@@ -186,9 +195,10 @@
     rising = (lane + 0.5) / half
     falling = 1.0 - rising
     row = lax.broadcasted_iota(jnp.int32, (third, 1), 0).astype(F32)
-    for j, (block, mid_out, side_out) in enumerate(
-        zip(blocks, (mid_out_0, mid_out_1, mid_out_2), (side_out_0, side_out_1, side_out_2))
-    ):
+    mids = []
+    fars = []
+    nears = []
+    for j, block in enumerate(blocks):
         knots = (row + 0.5) / third + j
         if j == 0:
             weight = 0.5 * knots * knots
@@ -202,19 +212,30 @@
         odd = by_table(odd, row_ref[6], row_ref[7])
         lower = (even + odd) * (weight * rising)
         upper = (even - odd) * (weight * falling)
-        side_out[:, :quarter] = lower[:, :quarter]
-        side_out[:, quarter:] = upper[:, quarter:]
-        mid_out[:, :quarter] = lower[:, quarter:]
-        mid_out[:, quarter:] = upper[:, :quarter]
+        far, near = swapped(odd_col, lower[:, :quarter], upper[:, quarter:])
+        fars.append(far)
+        nears.append(near)
+        mids.append(jnp.concatenate([lower[:, quarter:], upper[:, :quarter]], axis=1))
+    far_own_out[...] = fars[1]
+    near_own_out[...] = nears[1]
+    mid_own_out[...] = mids[1]
+    far_far_out[...], far_near_out[...] = swapped(odd_row, fars[0], fars[2])
+    near_far_out[...], near_near_out[...] = swapped(odd_row, nears[0], nears[2])
+    mid_far_out[...], mid_near_out[...] = swapped(odd_row, mids[0], mids[2])
 
 
 def whole(count):
     return [pl.BlockSpec(memory_space=pltpu.VMEM)] * count
 
 
-def passed_along(shard, axis, by):
-    length = lax.axis_size(axis)
-    return lax.ppermute(shard, axis, [(i, (i + by) % length) for i in range(length)])
+def exchanged(to_far, to_near, axis):
+    count = lax.axis_size(axis)
+    assert count % 2 == 0
+    far = [(i, (i - 1 + 2 * (i % 2)) % count) for i in range(count)]
+    near = [(i, (i + 1 - 2 * (i % 2)) % count) for i in range(count)]
+    from_far = lax.ppermute(to_far, axis, far)
+    from_near = lax.ppermute(to_near, axis, near)
+    return from_far, from_near
 
 
 def per_device(noise, root_spectrum):
@@ -224,6 +245,7 @@
     forward_table, back_table = (jnp.asarray(t) for t in column_tables(rows))
     mirror_table = jnp.asarray(mirror_tables(rows))
     limit = pltpu.CompilerParams(vmem_limit_bytes=24 * 1024 * 1024)
+    odd_col = lax.axis_index("tx") % 2 == 1
     mixed, crossed = pl.pallas_call(
         spectrum_kernel,
         out_shape=(jax.ShapeDtypeStruct((rows, cols // 2), F32), jax.ShapeDtypeStruct((rows, cols // 4), F32)),
@@ -233,19 +255,18 @@
         cost_estimate=pl.CostEstimate(flops=2 * 10**9, bytes_accessed=10**6, transcendentals=0),
         name="spectrum",
     )(root_spectrum)
-    from_left = passed_along(noise[:, block_cols - margin:], "tx", 1)
-    from_right = passed_along(noise[:, :margin], "tx", -1)
-    upper = passed_along(noise, "ty", 1)
-    lower = passed_along(noise, "ty", -1)
-    side = jnp.concatenate([from_left, from_right], axis=1)
-    upper_side = passed_along(side, "ty", 1)
-    lower_side = passed_along(side, "ty", -1)
+    to_far, to_near = swapped(odd_col, noise[:, :margin], noise[:, block_cols - margin:])
+    far, near = exchanged(to_far, to_near, "tx")
+    mid_far, mid_near = exchanged(noise, noise, "ty")
+    near_far, near_near = exchanged(near, near, "ty")
+    far_far, far_near = exchanged(far, far, "ty")
+    strip = jax.ShapeDtypeStruct((margin, margin), F32)
     block = jax.ShapeDtypeStruct((margin, block_cols), F32)
-    mid_0, mid_1, mid_2, side_0, side_1, side_2 = pl.pallas_call(
+    mid_far, mid, mid_near, far_far, far, far_near, near_far, near, near_near = pl.pallas_call(
         filter_kernel,
-        out_shape=(block,) * 6,
-        in_specs=whole(12),
-        out_specs=tuple(whole(6)),
+        out_shape=(block,) * 3 + (strip,) * 6,
+        in_specs=whole(15),
+        out_specs=tuple(whole(9)),
         scratch_shapes=[
             pltpu.VMEM((3, margin, block_cols), F32),
             pltpu.VMEM((3, margin, block_cols), F32),
@@ -254,17 +275,16 @@
         compiler_params=limit,
         cost_estimate=pl.CostEstimate(flops=4 * 10**9, bytes_accessed=10**7, transcendentals=0),
         name="filter",
-    )(upper, noise, lower, upper_side, side, lower_side, mixed, crossed, row_table, forward_table, back_table,
-      mirror_table)
-    side = side_1 + passed_along(side_0, "ty", -1) + passed_along(side_2, "ty", 1)
-    to_right = passed_along(side[:, margin:], "tx", 1)
-    to_left = passed_along(side[:, :margin], "tx", -1)
-    mid = mid_1 + passed_along(mid_0, "ty", -1) + passed_along(mid_2, "ty", 1)
-    return mid + jnp.concatenate([to_right, to_left], axis=1)
+    )(mid_far, noise, mid_near, far_far, far, far_near, near_far, near, near_near, mixed, crossed, row_table,
+      forward_table, back_table, mirror_table)
+    far_far, far_near = exchanged(far_far, far_near, "ty")
+    near_far, near_near = exchanged(near_far, near_near, "ty")
+    mid_far, mid_near = exchanged(mid_far, mid_near, "ty")
+    from_far, from_near = exchanged(far + far_far + far_near, near + near_far + near_near, "tx")
+    mid = mid + mid_far + mid_near
+    return mid + jnp.concatenate(swapped(odd_col, from_far, from_near), axis=1)
 
 
 def solution(mesh):
     placed = (P("ty", "tx"), P())
-    return jax.shard_map(
-        per_device, mesh=mesh, in_specs=placed, out_specs=P("ty", "tx"), check_vma=False
-    )
+    return jax.shard_map(per_device, mesh=mesh, in_specs=placed, out_specs=P("ty", "tx"), check_vma=False)

time: 33.7 us -> 35.8 us (1.062)
  starting transfers between devices: 15.8 us -> 20.3 us
  waiting for transfers between devices: 11.2 us -> 8.74 us
  local copies, waits for them, and re-layouts: 2.1 us -> 1.15 us
  other arithmetic: 0.71 us -> 1.65 us
    ppermute x12 -> x16, starting transfers between devices: 15.8 us -> 20.3 us  [the longest x8 14.5 us: exchanged(): from_far = lax.ppermute(to_far, axis, far)]
    ppermute x12 -> x16, waiting for transfers between devices: 11.2 us -> 8.74 us  [the longest x8 8.72 us: exchanged(): from_far = lax.ppermute(to_far, axis, far)]
    select_n x0 -> x2, other arithmetic: none -> 0.93 us  [swapped(): return (jnp.where(odd, second, first), jnp.where(odd, first, second))]
    slice x2 -> x0, local copies, waits for them, and re-layouts: 0.93 us -> none  [the longest x1 0.92 us: per_device(): from_right = passed_along(noise[:, :margin], 'tx', -1)]
    unnamed x13 -> x12, local copies, waits for them, and re-layouts: 1.16 us -> 1.15 us
  transfers between devices with their start and end apart: 12 -> 16, of which waited for: 8 -> 5; matrix products, arithmetic and copies ran while one was open for 0% -> 0% of each run, Pallas kernels for 4% -> 4%
where the time goes in v1:
time: 35.8 us; the launch traced here: 35.6 us
  starting transfers between devices  20.3 us (57%)
  waiting for transfers between devices  8.74 us (24%)
  Pallas kernels  3.74 us (10%)
  other arithmetic  1.65 us (5%)
  local copies, waits for them, and re-layouts  1.15 us (3%)
    ppermute x8, starting transfers between devices, exchanged(): from_far = lax.ppermute(to_far, axis, far)  14.5 us
    ppermute x8, waiting for transfers between devices, exchanged(): from_far = lax.ppermute(to_far, axis, far)  8.72 us
    ppermute x8, starting transfers between devices, exchanged(): from_near = lax.ppermute(to_near, axis, near)  5.81 us
    pallas_call x1, Pallas kernels, per_device(): pl.pallas_call(filter_kernel, out_shape=(block,) * 3 + (strip,) * 6, in_s...  2.33 us
    pallas_call x1, Pallas kernels, per_device(): pl.pallas_call(spectrum_kernel, out_shape=(jax.ShapeDtypeStruct((rows, co...  1.41 us
    unnamed x12, local copies, waits for them, and re-layouts  1.15 us
    select_n x2, other arithmetic, swapped(): return (jnp.where(odd, second, first), jnp.where(odd, first, second))  0.93 us
  transfers between devices with their start and end apart: 16, of which 5 were waited for; matrix products, arithmetic and copies ran while one was open for 0% of the time, Pallas kernels for 4%

profile of v1, /device:TPU:0, one launch (start us, length us, event | category | flops | bytes accessed | tf_op | source)
XLA Modules:
  0.0 35.6 jit_solution(12106251355918861293)
XLA Ops:
  0.0 0.9 %slice_select_fusion = (f32[128,128]{1,0:T(8,128)S(1)}, f32[128,128]{1,0:T(8,128)S(1)}) fusion(f32[128,256]{1,0:T(8,128)} %mid_own.1, pred[]{:T(512)S(6)} %eq.5), kind=kLoop, calls=%fused_computation.3 | loop fusion | flops 32768 | bytes 262145 | tf_op jit(solution)/shard_map/jit(_where)/select_n | solution.py:125
  0.9 3.1 %collective-permute-start.5 = (f32[128,128]{1,0:T(8,128)S(1)}, f32[128,128]{1,0:T(8,128)S(1)}, u32[]{:S(2)}, u32[]{:S(2)}) collective-permute-start(f32[128,128]{1,0:T(8,128)S(1)} %get-tuple-element.29), channel_id=1, source_target_pairs={{0,1},{1,0},{2,3},{3,2},{4,5},{5,4},{6,7},{7,6},{8,9},{9,8},{10,11... | collective-permute-start | bytes 196616 | tf_op jit(solution)/shard_map/ppermute | solution.py:237
  4.0 2.5 %collective-permute-start.2 = (f32[128,128]{1,0:T(8,128)S(1)}, f32[128,128]{1,0:T(8,128)S(1)}, u32[]{:S(2)}, u32[]{:S(2)}) collective-permute-start(f32[128,128]{1,0:T(8,128)S(1)} %get-tuple-element.30), channel_id=1, source_target_pairs={{0,3},{1,2},{2,1},{3,0},{4,7},{5,6},{6,5},{7,4},{8,11},{9,10},{10,... | collective-permute-start | bytes 196616 | tf_op jit(solution)/shard_map/ppermute | solution.py:236
  6.5 0.0 collective-permute-done.5.near_own
  6.5 0.0 collective-permute-start.7
  6.5 0.5 %collective-permute-start.1 = (f32[128,256]{1,0:T(8,128)S(1)}, f32[128,256]{1,0:T(8,128)S(1)}, u32[]{:S(2)}, u32[]{:S(2)}) collective-permute-start(f32[128,256]{1,0:T(8,128)S(1)} %copy-done), channel_id=1, source_target_pairs={{0,4},{4,0},{8,12},{12,8},{16,20},{20,16},{24,28},{28,24},{1,5},{5... | collective-permute-start | bytes 393224 | tf_op jit(solution)/shard_map/ppermute | solution.py:237
  7.0 2.3 %collective-permute-start = (f32[128,256]{1,0:T(8,128)S(1)}, f32[128,256]{1,0:T(8,128)S(1)}, u32[]{:S(2)}, u32[]{:S(2)}) collective-permute-start(f32[128,256]{1,0:T(8,128)S(1)} %copy-done), channel_id=1, source_target_pairs={{0,28},{4,8},{8,4},{12,16},{16,12},{20,24},{24,20},{28,0},{1,29},{... | collective-permute-start | bytes 393224 | tf_op jit(solution)/shard_map/ppermute | solution.py:236
  9.3 0.4 %collective-permute-start.6 = (f32[128,128]{1,0:T(8,128)S(1)}, f32[128,128]{1,0:T(8,128)S(1)}, u32[]{:S(2)}, u32[]{:S(2)}) collective-permute-start(f32[128,128]{1,0:T(8,128)S(1)} %collective-permute-done.5.near_own), channel_id=1, source_target_pairs={{0,28},{4,8},{8,4},{12,16},{16,12},{20,24},{24,20},{28,0},{1,29},{... | collective-permute-start | bytes 196616 | tf_op jit(solution)/shard_map/ppermute | solution.py:236
  9.7 0.5 %collective-permute-done.2.far_own = f32[128,128]{1,0:T(8,128)S(1)} collective-permute-done((f32[128,128]{1,0:T(8,128)S(1)}, f32[128,128]{1,0:T(8,128)S(1)}, u32[]{:S(2)}, u32[]{:S(2)}) %collective-permute-start.2) | collective-permute-done | bytes 65568 | tf_op jit(solution)/shard_map/ppermute | solution.py:236
  10.2 2.6 %collective-permute-start.3 = (f32[128,128]{1,0:T(8,128)S(1)}, f32[128,128]{1,0:T(8,128)S(1)}, u32[]{:S(2)}, u32[]{:S(2)}) collective-permute-start(f32[128,128]{1,0:T(8,128)S(1)} %collective-permute-done.2.far_own), channel_id=1, source_target_pairs={{0,28},{4,8},{8,4},{12,16},{16,12},{20,24},{24,20},{28,0},{1,29},{... | collective-permute-start | bytes 196616 | tf_op jit(solution)/shard_map/ppermute | solution.py:236
  12.7 1.1 %copy-done.1 = f32[384,512]{1,0:T(8,128)S(1)} copy-done((f32[384,512]{1,0:T(8,128)S(1)}, f32[384,512]{1,0:T(8,128)}, u32[]{:S(2)}) %copy-start.1) | copy-done | bytes 786456
  13.9 1.4 %spectrum.1 = (f32[384,256]{1,0:T(8,128)S(1)}, f32[384,128]{1,0:T(8,128)S(1)}) custom-call(f32[384,512]{1,0:T(8,128)S(1)} %copy-done.1), custom_call_target="tpu_custom_call" | custom-call | flops 2000000000 | bytes 1000000 | tf_op jit(solution)/shard_map/spectrum/pallas_call | solution.py:249
  15.3 0.8 %collective-permute-done.3.far_far = f32[128,128]{1,0:T(8,128)S(1)} collective-permute-done((f32[128,128]{1,0:T(8,128)S(1)}, f32[128,128]{1,0:T(8,128)S(1)}, u32[]{:S(2)}, u32[]{:S(2)}) %collective-permute-start.3) | collective-permute-done | bytes 65568 | tf_op jit(solution)/shard_map/ppermute | solution.py:236
  16.1 2.3 %filter.1 = (f32[128,256]{1,0:T(8,128)S(1)}, f32[128,256]{1,0:T(8,128)S(1)}, f32[128,256]{1,0:T(8,128)S(1)}, f32[128,128]{1,0:T(8,128)S(1)}, f32[128,128]{1,0:T(...) custom-call(f32[128,256]{1,0:T(8,128)S(1)} %collective-permute-done., ...), custom_call_target="tpu_custom_call" | custom-call | flops 4000000000 | bytes 10000000 | tf_op jit(solution)/shard_map/filter/pallas_call | solution.py:265
  18.5 1.6 %collective-permute-start.10 = (f32[128,128]{1,0:T(8,128)S(1)}, f32[128,128]{1,0:T(8,128)S(1)}, u32[]{:S(2)}, u32[]{:S(2)}) collective-permute-start(f32[128,128]{1,0:T(8,128)S(1)} %get-tuple-element.22), channel_id=1, source_target_pairs={{0,28},{4,8},{8,4},{12,16},{16,12},{20,24},{24,20},{28,0},{1,29},{... | collective-permute-start | bytes 196616 | tf_op jit(solution)/shard_map/ppermute | solution.py:236
  20.1 1.1 %collective-permute-start.13 = (f32[128,128]{1,0:T(8,128)S(1)}, f32[128,128]{1,0:T(8,128)S(1)}, u32[]{:S(2)}, u32[]{:S(2)}) collective-permute-start(f32[128,128]{1,0:T(8,128)S(1)} %get-tuple-element.25), channel_id=1, source_target_pairs={{0,28},{4,8},{8,4},{12,16},{16,12},{20,24},{24,20},{28,0},{1,29},{... | collective-permute-start | bytes 196616 | tf_op jit(solution)/shard_map/ppermute | solution.py:236
  21.2 0.3 collective-permute-start.14
  21.5 2.2 %collective-permute-done.10 = f32[128,128]{1,0:T(8,128)S(1)} collective-permute-done((f32[128,128]{1,0:T(8,128)S(1)}, f32[128,128]{1,0:T(8,128)S(1)}, u32[]{:S(2)}, u32[]{:S(2)}) %collective-permute-start.10) | collective-permute-done | bytes 65568 | tf_op jit(solution)/shard_map/ppermute | solution.py:236
  23.7 1.9 %collective-permute-start.12 = (f32[128,128]{1,0:T(8,128)S(1)}, f32[128,128]{1,0:T(8,128)S(1)}, u32[]{:S(2)}, u32[]{:S(2)}) collective-permute-start(f32[128,128]{1,0:T(8,128)S(1)} %add_add_fusion.1), channel_id=1, source_target_pairs={{0,1},{1,0},{2,3},{3,2},{4,5},{5,4},{6,7},{7,6},{8,9},{9,8},{10,11... | collective-permute-start | bytes 196616 | tf_op jit(solution)/shard_map/ppermute | solution.py:237
  25.6 3.2 %collective-permute-start.15 = (f32[128,128]{1,0:T(8,128)S(1)}, f32[128,128]{1,0:T(8,128)S(1)}, u32[]{:S(2)}, u32[]{:S(2)}) collective-permute-start(f32[128,128]{1,0:T(8,128)S(1)} %add_add_fusion), channel_id=1, source_target_pairs={{0,3},{1,2},{2,1},{3,0},{4,7},{5,6},{6,5},{7,4},{8,11},{9,10},{10,... | collective-permute-start | bytes 196616 | tf_op jit(solution)/shard_map/ppermute | solution.py:236
  28.8 0.9 %collective-permute-start.8 = (f32[128,256]{1,0:T(8,128)S(1)}, f32[128,256]{1,0:T(8,128)S(1)}, u32[]{:S(2)}, u32[]{:S(2)}) collective-permute-start(f32[128,256]{1,0:T(8,128)S(1)} %get-tuple-element.19), channel_id=1, source_target_pairs={{0,28},{4,8},{8,4},{12,16},{16,12},{20,24},{24,20},{28,0},{1,29},{... | collective-permute-start | bytes 393224 | tf_op jit(solution)/shard_map/ppermute | solution.py:236
  29.7 2.2 %collective-permute-done.15 = f32[128,128]{1,0:T(8,128)S(1)} collective-permute-done((f32[128,128]{1,0:T(8,128)S(1)}, f32[128,128]{1,0:T(8,128)S(1)}, u32[]{:S(2)}, u32[]{:S(2)}) %collective-permute-start.15) | collective-permute-done | bytes 65568 | tf_op jit(solution)/shard_map/ppermute | solution.py:236
  31.8 3.1 %collective-permute-done.8 = f32[128,256]{1,0:T(8,128)S(1)} collective-permute-done((f32[128,256]{1,0:T(8,128)S(1)}, f32[128,256]{1,0:T(8,128)S(1)}, u32[]{:S(2)}, u32[]{:S(2)}) %collective-permute-start.8) | collective-permute-done | bytes 131104 | tf_op jit(solution)/shard_map/ppermute | solution.py:236
  35.0 0.7 %maximum_add_fusion = f32[128,256]{1,0:T(8,128)} fusion(f32[128,128]{1,0:T(8,128)S(1)} %get-tuple-element.28, f32[128,128]{1,0:T(8,128)S(1)} %get-tuple-element.27, f32[128,256]{1,0:T(8,128)S(1)} %collective-permute-done.9, f32[128,256]{1,0:T(8,128)S(1)} %get-tuple-element.18, f32[128,256]{1,0:T(8,128)S(1)} %collective-permute-done.8), kind=kLoop, calls=%fused_computation | loop fusion | flops 131072 | bytes 655360 | tf_op jit(solution)/shard_map/add | solution.py:285
  (27 shorter events, 0.1 us)
Async XLA Ops:
  0.0 6.5 %copy-start = (f32[128,256]{1,0:T(8,128)S(1)}, f32[128,256]{1,0:T(8,128)}, u32[]{:S(2)}) copy-start(f32[128,256]{1,0:T(8,128)} %mid_own.1) | copy-start | bytes 393220
  0.9 5.6 %collective-permute-start.5 = (f32[128,128]{1,0:T(8,128)S(1)}, f32[128,128]{1,0:T(8,128)S(1)}, u32[]{:S(2)}, u32[]{:S(2)}) collective-permute-start(f32[128,128]{1,0:T(8,128)S(1)} %get-tuple-element.29), channel_id=1, source_target_pairs={{0,1},{1,0},{2,3},{3,2},{4,5},{5,4},{6,7},{7,6},{8,9},{9,8},{10,11... | collective-permute-start | bytes 196616 | tf_op jit(solution)/shard_map/ppermute | solution.py:237
  4.0 6.1 %collective-permute-start.2 = (f32[128,128]{1,0:T(8,128)S(1)}, f32[128,128]{1,0:T(8,128)S(1)}, u32[]{:S(2)}, u32[]{:S(2)}) collective-permute-start(f32[128,128]{1,0:T(8,128)S(1)} %get-tuple-element.30), channel_id=1, source_target_pairs={{0,3},{1,2},{2,1},{3,0},{4,7},{5,6},{6,5},{7,4},{8,11},{9,10},{10,... | collective-permute-start | bytes 196616 | tf_op jit(solution)/shard_map/ppermute | solution.py:236
  6.5 3.6 %collective-permute-start.7 = (f32[128,128]{1,0:T(8,128)S(1)}, f32[128,128]{1,0:T(8,128)S(1)}, u32[]{:S(2)}, u32[]{:S(2)}) collective-permute-start(f32[128,128]{1,0:T(8,128)S(1)} %collective-permute-done.5.near_own), channel_id=1, source_target_pairs={{0,4},{4,0},{8,12},{12,8},{16,20},{20,16},{24,28},{28,24},{1,5},{5... | collective-permute-start | bytes 196616 | tf_op jit(solution)/shard_map/ppermute | solution.py:237
  6.5 9.6 %collective-permute-start.1 = (f32[128,256]{1,0:T(8,128)S(1)}, f32[128,256]{1,0:T(8,128)S(1)}, u32[]{:S(2)}, u32[]{:S(2)}) collective-permute-start(f32[128,256]{1,0:T(8,128)S(1)} %copy-done), channel_id=1, source_target_pairs={{0,4},{4,0},{8,12},{12,8},{16,20},{20,16},{24,28},{28,24},{1,5},{5... | collective-permute-start | bytes 393224 | tf_op jit(solution)/shard_map/ppermute | solution.py:237
  7.0 9.1 %collective-permute-start = (f32[128,256]{1,0:T(8,128)S(1)}, f32[128,256]{1,0:T(8,128)S(1)}, u32[]{:S(2)}, u32[]{:S(2)}) collective-permute-start(f32[128,256]{1,0:T(8,128)S(1)} %copy-done), channel_id=1, source_target_pairs={{0,28},{4,8},{8,4},{12,16},{16,12},{20,24},{24,20},{28,0},{1,29},{... | collective-permute-start | bytes 393224 | tf_op jit(solution)/shard_map/ppermute | solution.py:236
  9.3 6.0 %collective-permute-start.6 = (f32[128,128]{1,0:T(8,128)S(1)}, f32[128,128]{1,0:T(8,128)S(1)}, u32[]{:S(2)}, u32[]{:S(2)}) collective-permute-start(f32[128,128]{1,0:T(8,128)S(1)} %collective-permute-done.5.near_own), channel_id=1, source_target_pairs={{0,28},{4,8},{8,4},{12,16},{16,12},{20,24},{24,20},{28,0},{1,29},{... | collective-permute-start | bytes 196616 | tf_op jit(solution)/shard_map/ppermute | solution.py:236
  10.2 5.1 %collective-permute-start.4 = (f32[128,128]{1,0:T(8,128)S(1)}, f32[128,128]{1,0:T(8,128)S(1)}, u32[]{:S(2)}, u32[]{:S(2)}) collective-permute-start(f32[128,128]{1,0:T(8,128)S(1)} %collective-permute-done.2.far_own), channel_id=1, source_target_pairs={{0,4},{4,0},{8,12},{12,8},{16,20},{20,16},{24,28},{28,24},{1,5},{5... | collective-permute-start | bytes 196616 | tf_op jit(solution)/shard_map/ppermute | solution.py:237
  10.2 5.9 %collective-permute-start.3 = (f32[128,128]{1,0:T(8,128)S(1)}, f32[128,128]{1,0:T(8,128)S(1)}, u32[]{:S(2)}, u32[]{:S(2)}) collective-permute-start(f32[128,128]{1,0:T(8,128)S(1)} %collective-permute-done.2.far_own), channel_id=1, source_target_pairs={{0,28},{4,8},{8,4},{12,16},{16,12},{20,24},{24,20},{28,0},{1,29},{... | collective-permute-start | bytes 196616 | tf_op jit(solution)/shard_map/ppermute | solution.py:236
  12.7 1.1 %copy-start.1 = (f32[384,512]{1,0:T(8,128)S(1)}, f32[384,512]{1,0:T(8,128)}, u32[]{:S(2)}) copy-start(f32[384,512]{1,0:T(8,128)} %root_ref.1) | copy-start | bytes 2359300
  13.9 2.2 %copy-start.2 = (bf16[8,256,256]{2,1,0:T(8,128)(2,1)S(1)}, bf16[8,256,256]{2,1,0:T(8,128)(2,1)}, u32[]{:S(2)}) copy-start(bf16[8,256,256]{2,1,0:T(8,128)(2,1)} %constant.26.clone.row_ref) | copy-start | bytes 3145732
  13.9 2.2 %copy-start.3 = (bf16[6,256,256]{2,1,0:T(8,128)(2,1)S(1)}, bf16[6,256,256]{2,1,0:T(8,128)(2,1)}, u32[]{:S(2)}) copy-start(bf16[6,256,256]{2,1,0:T(8,128)(2,1)} %constant.28.clone.back_ref) | copy-start | bytes 2359300
  13.9 2.2 %copy-start.4 = (bf16[6,256,256]{2,1,0:T(8,128)(2,1)S(1)}, bf16[6,256,256]{2,1,0:T(8,128)(2,1)}, u32[]{:S(2)}) copy-start(bf16[6,256,256]{2,1,0:T(8,128)(2,1)} %constant.27.clone.forward_ref) | copy-start | bytes 2359300
  13.9 2.3 %copy-start.5 = (bf16[2,256,256]{2,1,0:T(8,128)(2,1)S(1)}, bf16[2,256,256]{2,1,0:T(8,128)(2,1)}, u32[]{:S(2)}) copy-start(bf16[2,256,256]{2,1,0:T(8,128)(2,1)} %constant.29.clone.mirror_ref) | copy-start | bytes 786436
  18.5 5.2 %collective-permute-start.10 = (f32[128,128]{1,0:T(8,128)S(1)}, f32[128,128]{1,0:T(8,128)S(1)}, u32[]{:S(2)}, u32[]{:S(2)}) collective-permute-start(f32[128,128]{1,0:T(8,128)S(1)} %get-tuple-element.22), channel_id=1, source_target_pairs={{0,28},{4,8},{8,4},{12,16},{16,12},{20,24},{24,20},{28,0},{1,29},{... | collective-permute-start | bytes 196616 | tf_op jit(solution)/shard_map/ppermute | solution.py:236
  20.1 3.6 %collective-permute-start.11 = (f32[128,128]{1,0:T(8,128)S(1)}, f32[128,128]{1,0:T(8,128)S(1)}, u32[]{:S(2)}, u32[]{:S(2)}) collective-permute-start(f32[128,128]{1,0:T(8,128)S(1)} %get-tuple-element.23), channel_id=1, source_target_pairs={{0,4},{4,0},{8,12},{12,8},{16,20},{20,16},{24,28},{28,24},{1,5},{5... | collective-permute-start | bytes 196616 | tf_op jit(solution)/shard_map/ppermute | solution.py:237
  20.1 5.4 %collective-permute-start.13 = (f32[128,128]{1,0:T(8,128)S(1)}, f32[128,128]{1,0:T(8,128)S(1)}, u32[]{:S(2)}, u32[]{:S(2)}) collective-permute-start(f32[128,128]{1,0:T(8,128)S(1)} %get-tuple-element.25), channel_id=1, source_target_pairs={{0,28},{4,8},{8,4},{12,16},{16,12},{20,24},{24,20},{28,0},{1,29},{... | collective-permute-start | bytes 196616 | tf_op jit(solution)/shard_map/ppermute | solution.py:236
  21.2 4.4 %collective-permute-start.14 = (f32[128,128]{1,0:T(8,128)S(1)}, f32[128,128]{1,0:T(8,128)S(1)}, u32[]{:S(2)}, u32[]{:S(2)}) collective-permute-start(f32[128,128]{1,0:T(8,128)S(1)} %get-tuple-element.26), channel_id=1, source_target_pairs={{0,4},{4,0},{8,12},{12,8},{16,20},{20,16},{24,28},{28,24},{1,5},{5... | collective-permute-start | bytes 196616 | tf_op jit(solution)/shard_map/ppermute | solution.py:237
  23.7 5.9 %collective-permute-start.12 = (f32[128,128]{1,0:T(8,128)S(1)}, f32[128,128]{1,0:T(8,128)S(1)}, u32[]{:S(2)}, u32[]{:S(2)}) collective-permute-start(f32[128,128]{1,0:T(8,128)S(1)} %add_add_fusion.1), channel_id=1, source_target_pairs={{0,1},{1,0},{2,3},{3,2},{4,5},{5,4},{6,7},{7,6},{8,9},{9,8},{10,11... | collective-permute-start | bytes 196616 | tf_op jit(solution)/shard_map/ppermute | solution.py:237
  25.6 6.2 %collective-permute-start.15 = (f32[128,128]{1,0:T(8,128)S(1)}, f32[128,128]{1,0:T(8,128)S(1)}, u32[]{:S(2)}, u32[]{:S(2)}) collective-permute-start(f32[128,128]{1,0:T(8,128)S(1)} %add_add_fusion), channel_id=1, source_target_pairs={{0,3},{1,2},{2,1},{3,0},{4,7},{5,6},{6,5},{7,4},{8,11},{9,10},{10,... | collective-permute-start | bytes 196616 | tf_op jit(solution)/shard_map/ppermute | solution.py:236
  28.8 6.2 %collective-permute-start.8 = (f32[128,256]{1,0:T(8,128)S(1)}, f32[128,256]{1,0:T(8,128)S(1)}, u32[]{:S(2)}, u32[]{:S(2)}) collective-permute-start(f32[128,256]{1,0:T(8,128)S(1)} %get-tuple-element.19), channel_id=1, source_target_pairs={{0,28},{4,8},{8,4},{12,16},{16,12},{20,24},{24,20},{28,0},{1,29},{... | collective-permute-start | bytes 393224 | tf_op jit(solution)/shard_map/ppermute | solution.py:236
  29.7 5.3 %collective-permute-start.9 = (f32[128,256]{1,0:T(8,128)S(1)}, f32[128,256]{1,0:T(8,128)S(1)}, u32[]{:S(2)}, u32[]{:S(2)}) collective-permute-start(f32[128,256]{1,0:T(8,128)S(1)} %get-tuple-element.20), channel_id=1, source_target_pairs={{0,4},{4,0},{8,12},{12,8},{16,20},{20,16},{24,28},{28,24},{1,5},{5... | collective-permute-start | bytes 393224 | tf_op jit(solution)/shard_map/ppermute | solution.py:237

commit v2 on v1

--- a/solution.py
+++ b/solution.py
@@ -125,21 +125,19 @@
     return jnp.where(odd, second, first), jnp.where(odd, first, second)
 
 
-def filter_kernel(mid_far, mid_own, mid_near, far_far, far_own, far_near, near_far, near_own, near_near, mixed_ref,
+def filter_kernel(mid_far, mid_own, mid_near, left_far, left_own, left_near, right_far, right_own, right_near, mixed_ref,
                   crossed_ref, row_ref, forward_ref, back_ref, mirror_ref, mid_far_out, mid_own_out, mid_near_out,
-                  far_far_out, far_own_out, far_near_out, near_far_out, near_own_out, near_near_out, real_ref, imag_ref,
+                  left_far_out, left_own_out, left_near_out, right_far_out, right_own_out, right_near_out, real_ref, imag_ref,
                   spec_ref):
     third, half = mid_own.shape
     quarter = half // 2
     root_three = math.sqrt(3.0) / 2.0
     odd_row = lax.axis_index("ty") % 2 == 1
-    odd_col = lax.axis_index("tx") % 2 == 1
     mid_0, mid_2 = swapped(odd_row, mid_far[...], mid_near[...])
-    far_0, far_2 = swapped(odd_row, far_far[...], far_near[...])
-    near_0, near_2 = swapped(odd_row, near_far[...], near_near[...])
-    parts = ((mid_0, far_0, near_0), (mid_own[...], far_own[...], near_own[...]), (mid_2, far_2, near_2))
-    for j, (mid, far, near) in enumerate(parts):
-        left, right = swapped(odd_col, far, near)
+    left_0, left_2 = swapped(odd_row, left_far[...], left_near[...])
+    right_0, right_2 = swapped(odd_row, right_far[...], right_near[...])
+    parts = ((mid_0, left_0, right_0), (mid_own[...], left_own[...], right_own[...]), (mid_2, left_2, right_2))
+    for j, (mid, left, right) in enumerate(parts):
         first = mid[:, :quarter]
         second = mid[:, quarter:]
         even = jnp.concatenate([left + second, first + right], axis=1)
@@ -196,8 +194,8 @@
     falling = 1.0 - rising
     row = lax.broadcasted_iota(jnp.int32, (third, 1), 0).astype(F32)
     mids = []
-    fars = []
-    nears = []
+    lefts = []
+    rights = []
     for j, block in enumerate(blocks):
         knots = (row + 0.5) / third + j
         if j == 0:
@@ -212,20 +210,24 @@
         odd = by_table(odd, row_ref[6], row_ref[7])
         lower = (even + odd) * (weight * rising)
         upper = (even - odd) * (weight * falling)
-        far, near = swapped(odd_col, lower[:, :quarter], upper[:, quarter:])
-        fars.append(far)
-        nears.append(near)
+        lefts.append(lower[:, :quarter])
+        rights.append(upper[:, quarter:])
         mids.append(jnp.concatenate([lower[:, quarter:], upper[:, :quarter]], axis=1))
-    far_own_out[...] = fars[1]
-    near_own_out[...] = nears[1]
+    left_own_out[...] = lefts[1]
+    right_own_out[...] = rights[1]
     mid_own_out[...] = mids[1]
-    far_far_out[...], far_near_out[...] = swapped(odd_row, fars[0], fars[2])
-    near_far_out[...], near_near_out[...] = swapped(odd_row, nears[0], nears[2])
+    left_far_out[...], left_near_out[...] = swapped(odd_row, lefts[0], lefts[2])
+    right_far_out[...], right_near_out[...] = swapped(odd_row, rights[0], rights[2])
     mid_far_out[...], mid_near_out[...] = swapped(odd_row, mids[0], mids[2])
 
 
 def whole(count):
     return [pl.BlockSpec(memory_space=pltpu.VMEM)] * count
+
+
+def passed_along(shard, axis, by):
+    count = lax.axis_size(axis)
+    return lax.ppermute(shard, axis, [(i, (i + by) % count) for i in range(count)])
 
 
 def exchanged(to_far, to_near, axis):
@@ -245,7 +247,6 @@
     forward_table, back_table = (jnp.asarray(t) for t in column_tables(rows))
     mirror_table = jnp.asarray(mirror_tables(rows))
     limit = pltpu.CompilerParams(vmem_limit_bytes=24 * 1024 * 1024)
-    odd_col = lax.axis_index("tx") % 2 == 1
     mixed, crossed = pl.pallas_call(
         spectrum_kernel,
         out_shape=(jax.ShapeDtypeStruct((rows, cols // 2), F32), jax.ShapeDtypeStruct((rows, cols // 4), F32)),
@@ -255,14 +256,14 @@
         cost_estimate=pl.CostEstimate(flops=2 * 10**9, bytes_accessed=10**6, transcendentals=0),
         name="spectrum",
     )(root_spectrum)
-    to_far, to_near = swapped(odd_col, noise[:, :margin], noise[:, block_cols - margin:])
-    far, near = exchanged(to_far, to_near, "tx")
+    left = passed_along(noise[:, block_cols - margin:], "tx", 1)
+    right = passed_along(noise[:, :margin], "tx", -1)
     mid_far, mid_near = exchanged(noise, noise, "ty")
-    near_far, near_near = exchanged(near, near, "ty")
-    far_far, far_near = exchanged(far, far, "ty")
+    left_far, left_near = exchanged(left, left, "ty")
+    right_far, right_near = exchanged(right, right, "ty")
     strip = jax.ShapeDtypeStruct((margin, margin), F32)
     block = jax.ShapeDtypeStruct((margin, block_cols), F32)
-    mid_far, mid, mid_near, far_far, far, far_near, near_far, near, near_near = pl.pallas_call(
+    mid_far, mid, mid_near, left_far, left_own, left_near, right_far, right, right_near = pl.pallas_call(
         filter_kernel,
         out_shape=(block,) * 3 + (strip,) * 6,
         in_specs=whole(15),
@@ -275,14 +276,15 @@
         compiler_params=limit,
         cost_estimate=pl.CostEstimate(flops=4 * 10**9, bytes_accessed=10**7, transcendentals=0),
         name="filter",
-    )(mid_far, noise, mid_near, far_far, far, far_near, near_far, near, near_near, mixed, crossed, row_table,
-      forward_table, back_table, mirror_table)
-    far_far, far_near = exchanged(far_far, far_near, "ty")
-    near_far, near_near = exchanged(near_far, near_near, "ty")
+    )(mid_far, noise, mid_near, left_far, left, left_near, right_far, right, right_near, mixed, crossed,
+      row_table, forward_table, back_table, mirror_table)
+    right_far, right_near = exchanged(right_far, right_near, "ty")
+    left_far, left_near = exchanged(left_far, left_near, "ty")
     mid_far, mid_near = exchanged(mid_far, mid_near, "ty")
-    from_far, from_near = exchanged(far + far_far + far_near, near + near_far + near_near, "tx")
+    left = passed_along(right + right_far + right_near, "tx", 1)
+    right = passed_along(left_own + left_far + left_near, "tx", -1)
     mid = mid + mid_far + mid_near
-    return mid + jnp.concatenate(swapped(odd_col, from_far, from_near), axis=1)
+    return mid + jnp.concatenate([left, right], axis=1)
 
 
 def solution(mesh):

time: 35.8 us -> 33.3 us (0.930)
  waiting for transfers between devices: 8.74 us -> 7.1 us
  other arithmetic: 1.65 us -> 0.71 us
  local copies, waits for them, and re-layouts: 1.15 us -> 2.07 us
  starting transfers between devices: 20.3 us -> 19.4 us
    ppermute x0 -> x4, starting transfers between devices: none -> 9.29 us  [passed_along(): lax.ppermute(shard, axis, [(i, (i + by) % count) for i in range(count)])]
    ppermute x8 -> x6, waiting for transfers between devices: 8.72 us -> 2.15 us  [exchanged(): from_far = lax.ppermute(to_far, axis, far)]
    ppermute x8 -> x6, starting transfers between devices: 5.81 us -> 0.55 us  [exchanged(): from_near = lax.ppermute(to_near, axis, near)]
    ppermute x0 -> x4, waiting for transfers between devices: none -> 4.94 us  [passed_along(): lax.ppermute(shard, axis, [(i, (i + by) % count) for i in range(count)])]
    ppermute x8 -> x6, starting transfers between devices: 14.5 us -> 9.6 us  [exchanged(): from_far = lax.ppermute(to_far, axis, far)]
    select_n x2 -> x0, other arithmetic: 0.93 us -> none  [swapped(): return (jnp.where(odd, second, first), jnp.where(odd, first, second))]
    slice x0 -> x1, local copies, waits for them, and re-layouts: none -> 0.92 us  [per_device(): right = passed_along(noise[:, :margin], 'tx', -1)]
  transfers between devices with their start and end apart: 16 -> 16, of which waited for: 5 -> 6; matrix products, arithmetic and copies ran while one was open for 0% -> 0% of each run, Pallas kernels for 4% -> 4%
where the time goes in v2:
time: 33.3 us; the launch traced here: 33.2 us
  starting transfers between devices  19.4 us (58%)
  waiting for transfers between devices  7.1 us (21%)
  Pallas kernels  3.73 us (11%)
  local copies, waits for them, and re-layouts  2.07 us (6%)
  other arithmetic  0.71 us (2%)
    ppermute x6, starting transfers between devices, exchanged(): from_far = lax.ppermute(to_far, axis, far)  9.6 us
    ppermute x4, starting transfers between devices, passed_along(): lax.ppermute(shard, axis, [(i, (i + by) % count) for i in range(count)])  9.29 us
    ppermute x4, waiting for transfers between devices, passed_along(): lax.ppermute(shard, axis, [(i, (i + by) % count) for i in range(count)])  4.94 us
    pallas_call x1, Pallas kernels, per_device(): pl.pallas_call(filter_kernel, out_shape=(block,) * 3 + (strip,) * 6, in_s...  2.32 us
    ppermute x6, waiting for transfers between devices, exchanged(): from_far = lax.ppermute(to_far, axis, far)  2.15 us
    pallas_call x1, Pallas kernels, per_device(): pl.pallas_call(spectrum_kernel, out_shape=(jax.ShapeDtypeStruct((rows, co...  1.41 us
    unnamed x12, local copies, waits for them, and re-layouts  1.15 us
    slice x1, local copies, waits for them, and re-layouts, per_device(): right = passed_along(noise[:, :margin], 'tx', -1)  0.92 us
  transfers between devices with their start and end apart: 16, of which 6 were waited for; matrix products, arithmetic and copies ran while one was open for 0% of the time, Pallas kernels for 4%

profile of v2, /device:TPU:0, one launch (start us, length us, event | category | flops | bytes accessed | tf_op | source)
XLA Modules:
  0.0 33.2 jit_solution(14131489408251868205)
XLA Ops:
  0.0 0.9 %fusion = (f32[128,128]{1,0:T(8,128)S(1)}, f32[128,128]{1,0:T(8,128)S(1)}) fusion(f32[128,256]{1,0:T(8,128)} %mid_own.1), kind=kLoop, calls=%fused_computation.3 | loop fusion | bytes 262144 | tf_op jit(solution)/shard_map/slice | solution.py:260
  0.9 5.1 %collective-permute-start.5 = (f32[128,128]{1,0:T(8,128)S(1)}, f32[128,128]{1,0:T(8,128)S(1)}, u32[]{:S(2)}, u32[]{:S(2)}) collective-permute-start(f32[128,128]{1,0:T(8,128)S(1)} %get-tuple-element.27), channel_id=1, source_target_pairs={{0,3},{1,0},{2,1},{3,2},{4,7},{5,4},{6,5},{7,6},{8,11},{9,8},{10,9... | collective-permute-start | bytes 196616 | tf_op jit(solution)/shard_map/ppermute | solution.py:230
  6.1 2.0 %collective-permute-done.5.right_own = f32[128,128]{1,0:T(8,128)S(1)} collective-permute-done((f32[128,128]{1,0:T(8,128)S(1)}, f32[128,128]{1,0:T(8,128)S(1)}, u32[]{:S(2)}, u32[]{:S(2)}) %collective-permute-start.5) | collective-permute-done | bytes 65568 | tf_op jit(solution)/shard_map/ppermute | solution.py:230
  8.1 0.5 %collective-permute-start.1 = (f32[128,256]{1,0:T(8,128)S(1)}, f32[128,256]{1,0:T(8,128)S(1)}, u32[]{:S(2)}, u32[]{:S(2)}) collective-permute-start(f32[128,256]{1,0:T(8,128)S(1)} %copy-done), channel_id=1, source_target_pairs={{0,4},{4,0},{8,12},{12,8},{16,20},{20,16},{24,28},{28,24},{1,5},{5... | collective-permute-start | bytes 393224 | tf_op jit(solution)/shard_map/ppermute | solution.py:239
  8.6 2.1 %collective-permute-start = (f32[128,256]{1,0:T(8,128)S(1)}, f32[128,256]{1,0:T(8,128)S(1)}, u32[]{:S(2)}, u32[]{:S(2)}) collective-permute-start(f32[128,256]{1,0:T(8,128)S(1)} %copy-done), channel_id=1, source_target_pairs={{0,28},{4,8},{8,4},{12,16},{16,12},{20,24},{24,20},{28,0},{1,29},{... | collective-permute-start | bytes 393224 | tf_op jit(solution)/shard_map/ppermute | solution.py:238
  10.7 0.6 %collective-permute-start.6 = (f32[128,128]{1,0:T(8,128)S(1)}, f32[128,128]{1,0:T(8,128)S(1)}, u32[]{:S(2)}, u32[]{:S(2)}) collective-permute-start(f32[128,128]{1,0:T(8,128)S(1)} %collective-permute-done.5.right_own), channel_id=1, source_target_pairs={{0,28},{4,8},{8,4},{12,16},{16,12},{20,24},{24,20},{28,0},{1,29},{... | collective-permute-start | bytes 196616 | tf_op jit(solution)/shard_map/ppermute | solution.py:238
  11.3 0.9 %collective-permute-done.2.left_own = f32[128,128]{1,0:T(8,128)S(1)} collective-permute-done((f32[128,128]{1,0:T(8,128)S(1)}, f32[128,128]{1,0:T(8,128)S(1)}, u32[]{:S(2)}, u32[]{:S(2)}) %collective-permute-start.2) | collective-permute-done | bytes 65568 | tf_op jit(solution)/shard_map/ppermute | solution.py:230
  12.1 0.0 collective-permute-start.4
  12.1 0.0 collective-permute-done.7.right_near
  12.1 2.6 %collective-permute-start.3 = (f32[128,128]{1,0:T(8,128)S(1)}, f32[128,128]{1,0:T(8,128)S(1)}, u32[]{:S(2)}, u32[]{:S(2)}) collective-permute-start(f32[128,128]{1,0:T(8,128)S(1)} %collective-permute-done.2.left_own), channel_id=1, source_target_pairs={{0,28},{4,8},{8,4},{12,16},{16,12},{20,24},{24,20},{28,0},{1,29},{... | collective-permute-start | bytes 196616 | tf_op jit(solution)/shard_map/ppermute | solution.py:238
  14.7 1.1 %copy-done.1 = f32[384,512]{1,0:T(8,128)S(1)} copy-done((f32[384,512]{1,0:T(8,128)S(1)}, f32[384,512]{1,0:T(8,128)}, u32[]{:S(2)}) %copy-start.1) | copy-done | bytes 786456
  15.8 1.4 %spectrum.1 = (f32[384,256]{1,0:T(8,128)S(1)}, f32[384,128]{1,0:T(8,128)S(1)}) custom-call(f32[384,512]{1,0:T(8,128)S(1)} %copy-done.1), custom_call_target="tpu_custom_call" | custom-call | flops 2000000000 | bytes 1000000 | tf_op jit(solution)/shard_map/spectrum/pallas_call | solution.py:250
  17.3 0.6 %collective-permute-done.3.left_far = f32[128,128]{1,0:T(8,128)S(1)} collective-permute-done((f32[128,128]{1,0:T(8,128)S(1)}, f32[128,128]{1,0:T(8,128)S(1)}, u32[]{:S(2)}, u32[]{:S(2)}) %collective-permute-start.3) | collective-permute-done | bytes 65568 | tf_op jit(solution)/shard_map/ppermute | solution.py:238
  17.9 2.3 %filter.1 = (f32[128,256]{1,0:T(8,128)S(1)}, f32[128,256]{1,0:T(8,128)S(1)}, f32[128,256]{1,0:T(8,128)S(1)}, f32[128,128]{1,0:T(8,128)S(1)}, f32[128,128]{1,0:T(...) custom-call(f32[128,256]{1,0:T(8,128)S(1)} %collective-permute-done., ...), custom_call_target="tpu_custom_call" | custom-call | flops 4000000000 | bytes 10000000 | tf_op jit(solution)/shard_map/filter/pallas_call | solution.py:266
  20.3 1.5 %collective-permute-start.10 = (f32[128,128]{1,0:T(8,128)S(1)}, f32[128,128]{1,0:T(8,128)S(1)}, u32[]{:S(2)}, u32[]{:S(2)}) collective-permute-start(f32[128,128]{1,0:T(8,128)S(1)} %get-tuple-element.22), channel_id=1, source_target_pairs={{0,28},{4,8},{8,4},{12,16},{16,12},{20,24},{24,20},{28,0},{1,29},{... | collective-permute-start | bytes 196616 | tf_op jit(solution)/shard_map/ppermute | solution.py:238
  21.7 1.3 %collective-permute-start.13 = (f32[128,128]{1,0:T(8,128)S(1)}, f32[128,128]{1,0:T(8,128)S(1)}, u32[]{:S(2)}, u32[]{:S(2)}) collective-permute-start(f32[128,128]{1,0:T(8,128)S(1)} %get-tuple-element.25), channel_id=1, source_target_pairs={{0,28},{4,8},{8,4},{12,16},{16,12},{20,24},{24,20},{28,0},{1,29},{... | collective-permute-start | bytes 196616 | tf_op jit(solution)/shard_map/ppermute | solution.py:238
  23.0 0.0 collective-permute-start.14
  23.0 1.7 %collective-permute-start.8 = (f32[128,256]{1,0:T(8,128)S(1)}, f32[128,256]{1,0:T(8,128)S(1)}, u32[]{:S(2)}, u32[]{:S(2)}) collective-permute-start(f32[128,256]{1,0:T(8,128)S(1)} %get-tuple-element.19), channel_id=1, source_target_pairs={{0,28},{4,8},{8,4},{12,16},{16,12},{20,24},{24,20},{28,0},{1,29},{... | collective-permute-start | bytes 393224 | tf_op jit(solution)/shard_map/ppermute | solution.py:238
  24.7 0.6 %collective-permute-done.10 = f32[128,128]{1,0:T(8,128)S(1)} collective-permute-done((f32[128,128]{1,0:T(8,128)S(1)}, f32[128,128]{1,0:T(8,128)S(1)}, u32[]{:S(2)}, u32[]{:S(2)}) %collective-permute-start.10) | collective-permute-done | bytes 65568 | tf_op jit(solution)/shard_map/ppermute | solution.py:238
  25.3 0.2 collective-permute-start.12
  25.5 1.0 %collective-permute-done.13 = f32[128,128]{1,0:T(8,128)S(1)} collective-permute-done((f32[128,128]{1,0:T(8,128)S(1)}, f32[128,128]{1,0:T(8,128)S(1)}, u32[]{:S(2)}, u32[]{:S(2)}) %collective-permute-start.13) | collective-permute-done | bytes 65568 | tf_op jit(solution)/shard_map/ppermute | solution.py:238
  26.5 3.9 %collective-permute-start.15 = (f32[128,128]{1,0:T(8,128)S(1)}, f32[128,128]{1,0:T(8,128)S(1)}, u32[]{:S(2)}, u32[]{:S(2)}) collective-permute-start(f32[128,128]{1,0:T(8,128)S(1)} %add_add_fusion), channel_id=1, source_target_pairs={{0,3},{1,0},{2,1},{3,2},{4,7},{5,4},{6,5},{7,6},{8,11},{9,8},{10,9... | collective-permute-start | bytes 196616 | tf_op jit(solution)/shard_map/ppermute | solution.py:230
  30.4 2.0 %collective-permute-done.12 = f32[128,128]{1,0:T(8,128)S(1)} collective-permute-done((f32[128,128]{1,0:T(8,128)S(1)}, f32[128,128]{1,0:T(8,128)S(1)}, u32[]{:S(2)}, u32[]{:S(2)}) %collective-permute-start.12) | collective-permute-done | bytes 65568 | tf_op jit(solution)/shard_map/ppermute | solution.py:230
  32.5 0.7 %maximum_add_fusion = f32[128,256]{1,0:T(8,128)} fusion(f32[128,128]{1,0:T(8,128)S(1)} %collective-permute-done.15, f32[128,128]{1,0:T(8,128)S(1)} %collective-permute-done.12, f32[128,256]{1,0:T(8,128)S(1)} %collective-permute-done.9, f32[128,256]{1,0:T(8,128)S(1)} %get-tuple-element.18, f32[128,256]{1,0:T(8,128)S(1)} %collective-permute-done.8), kind=kLoop, calls=%fused_computation | loop fusion | flops 131072 | bytes 655360 | tf_op jit(solution)/shard_map/add | solution.py:287
  (26 shorter events, 0.1 us)
Async XLA Ops:
  0.0 8.1 %copy-start = (f32[128,256]{1,0:T(8,128)S(1)}, f32[128,256]{1,0:T(8,128)}, u32[]{:S(2)}) copy-start(f32[128,256]{1,0:T(8,128)} %mid_own.1) | copy-start | bytes 393220
  0.9 7.2 %collective-permute-start.5 = (f32[128,128]{1,0:T(8,128)S(1)}, f32[128,128]{1,0:T(8,128)S(1)}, u32[]{:S(2)}, u32[]{:S(2)}) collective-permute-start(f32[128,128]{1,0:T(8,128)S(1)} %get-tuple-element.27), channel_id=1, source_target_pairs={{0,3},{1,0},{2,1},{3,2},{4,7},{5,4},{6,5},{7,6},{8,11},{9,8},{10,9... | collective-permute-start | bytes 196616 | tf_op jit(solution)/shard_map/ppermute | solution.py:230
  6.1 6.1 %collective-permute-start.2 = (f32[128,128]{1,0:T(8,128)S(1)}, f32[128,128]{1,0:T(8,128)S(1)}, u32[]{:S(2)}, u32[]{:S(2)}) collective-permute-start(f32[128,128]{1,0:T(8,128)S(1)} %get-tuple-element.28), channel_id=1, source_target_pairs={{0,1},{1,2},{2,3},{3,0},{4,5},{5,6},{6,7},{7,4},{8,9},{9,10},{10,1... | collective-permute-start | bytes 196616 | tf_op jit(solution)/shard_map/ppermute | solution.py:230
  8.1 4.0 %collective-permute-start.7 = (f32[128,128]{1,0:T(8,128)S(1)}, f32[128,128]{1,0:T(8,128)S(1)}, u32[]{:S(2)}, u32[]{:S(2)}) collective-permute-start(f32[128,128]{1,0:T(8,128)S(1)} %collective-permute-done.5.right_own), channel_id=1, source_target_pairs={{0,4},{4,0},{8,12},{12,8},{16,20},{20,16},{24,28},{28,24},{1,5},{5... | collective-permute-start | bytes 196616 | tf_op jit(solution)/shard_map/ppermute | solution.py:239
  8.1 9.8 %collective-permute-start.1 = (f32[128,256]{1,0:T(8,128)S(1)}, f32[128,256]{1,0:T(8,128)S(1)}, u32[]{:S(2)}, u32[]{:S(2)}) collective-permute-start(f32[128,256]{1,0:T(8,128)S(1)} %copy-done), channel_id=1, source_target_pairs={{0,4},{4,0},{8,12},{12,8},{16,20},{20,16},{24,28},{28,24},{1,5},{5... | collective-permute-start | bytes 393224 | tf_op jit(solution)/shard_map/ppermute | solution.py:239
  8.6 9.3 %collective-permute-start = (f32[128,256]{1,0:T(8,128)S(1)}, f32[128,256]{1,0:T(8,128)S(1)}, u32[]{:S(2)}, u32[]{:S(2)}) collective-permute-start(f32[128,256]{1,0:T(8,128)S(1)} %copy-done), channel_id=1, source_target_pairs={{0,28},{4,8},{8,4},{12,16},{16,12},{20,24},{24,20},{28,0},{1,29},{... | collective-permute-start | bytes 393224 | tf_op jit(solution)/shard_map/ppermute | solution.py:238
  10.7 6.6 %collective-permute-start.6 = (f32[128,128]{1,0:T(8,128)S(1)}, f32[128,128]{1,0:T(8,128)S(1)}, u32[]{:S(2)}, u32[]{:S(2)}) collective-permute-start(f32[128,128]{1,0:T(8,128)S(1)} %collective-permute-done.5.right_own), channel_id=1, source_target_pairs={{0,28},{4,8},{8,4},{12,16},{16,12},{20,24},{24,20},{28,0},{1,29},{... | collective-permute-start | bytes 196616 | tf_op jit(solution)/shard_map/ppermute | solution.py:238
  12.1 5.1 %collective-permute-start.4 = (f32[128,128]{1,0:T(8,128)S(1)}, f32[128,128]{1,0:T(8,128)S(1)}, u32[]{:S(2)}, u32[]{:S(2)}) collective-permute-start(f32[128,128]{1,0:T(8,128)S(1)} %collective-permute-done.2.left_own), channel_id=1, source_target_pairs={{0,4},{4,0},{8,12},{12,8},{16,20},{20,16},{24,28},{28,24},{1,5},{5... | collective-permute-start | bytes 196616 | tf_op jit(solution)/shard_map/ppermute | solution.py:239
  12.1 5.8 %collective-permute-start.3 = (f32[128,128]{1,0:T(8,128)S(1)}, f32[128,128]{1,0:T(8,128)S(1)}, u32[]{:S(2)}, u32[]{:S(2)}) collective-permute-start(f32[128,128]{1,0:T(8,128)S(1)} %collective-permute-done.2.left_own), channel_id=1, source_target_pairs={{0,28},{4,8},{8,4},{12,16},{16,12},{20,24},{24,20},{28,0},{1,29},{... | collective-permute-start | bytes 196616 | tf_op jit(solution)/shard_map/ppermute | solution.py:238
  14.7 1.1 %copy-start.1 = (f32[384,512]{1,0:T(8,128)S(1)}, f32[384,512]{1,0:T(8,128)}, u32[]{:S(2)}) copy-start(f32[384,512]{1,0:T(8,128)} %root_ref.1) | copy-start | bytes 2359300
  15.8 2.1 %copy-start.2 = (bf16[8,256,256]{2,1,0:T(8,128)(2,1)S(1)}, bf16[8,256,256]{2,1,0:T(8,128)(2,1)}, u32[]{:S(2)}) copy-start(bf16[8,256,256]{2,1,0:T(8,128)(2,1)} %constant.8.clone.row_ref) | copy-start | bytes 3145732
  15.8 2.1 %copy-start.3 = (bf16[6,256,256]{2,1,0:T(8,128)(2,1)S(1)}, bf16[6,256,256]{2,1,0:T(8,128)(2,1)}, u32[]{:S(2)}) copy-start(bf16[6,256,256]{2,1,0:T(8,128)(2,1)} %constant.10.clone.back_ref) | copy-start | bytes 2359300
  15.8 2.1 %copy-start.4 = (bf16[6,256,256]{2,1,0:T(8,128)(2,1)S(1)}, bf16[6,256,256]{2,1,0:T(8,128)(2,1)}, u32[]{:S(2)}) copy-start(bf16[6,256,256]{2,1,0:T(8,128)(2,1)} %constant.9.clone.forward_ref) | copy-start | bytes 2359300
  15.8 2.1 %copy-start.5 = (bf16[2,256,256]{2,1,0:T(8,128)(2,1)S(1)}, bf16[2,256,256]{2,1,0:T(8,128)(2,1)}, u32[]{:S(2)}) copy-start(bf16[2,256,256]{2,1,0:T(8,128)(2,1)} %constant.11.clone.mirror_ref) | copy-start | bytes 786436
  20.3 5.0 %collective-permute-start.10 = (f32[128,128]{1,0:T(8,128)S(1)}, f32[128,128]{1,0:T(8,128)S(1)}, u32[]{:S(2)}, u32[]{:S(2)}) collective-permute-start(f32[128,128]{1,0:T(8,128)S(1)} %get-tuple-element.22), channel_id=1, source_target_pairs={{0,28},{4,8},{8,4},{12,16},{16,12},{20,24},{24,20},{28,0},{1,29},{... | collective-permute-start | bytes 196616 | tf_op jit(solution)/shard_map/ppermute | solution.py:238
  21.7 3.5 %collective-permute-start.11 = (f32[128,128]{1,0:T(8,128)S(1)}, f32[128,128]{1,0:T(8,128)S(1)}, u32[]{:S(2)}, u32[]{:S(2)}) collective-permute-start(f32[128,128]{1,0:T(8,128)S(1)} %get-tuple-element.23), channel_id=1, source_target_pairs={{0,4},{4,0},{8,12},{12,8},{16,20},{20,16},{24,28},{28,24},{1,5},{5... | collective-permute-start | bytes 196616 | tf_op jit(solution)/shard_map/ppermute | solution.py:239
  21.7 4.8 %collective-permute-start.13 = (f32[128,128]{1,0:T(8,128)S(1)}, f32[128,128]{1,0:T(8,128)S(1)}, u32[]{:S(2)}, u32[]{:S(2)}) collective-permute-start(f32[128,128]{1,0:T(8,128)S(1)} %get-tuple-element.25), channel_id=1, source_target_pairs={{0,28},{4,8},{8,4},{12,16},{16,12},{20,24},{24,20},{28,0},{1,29},{... | collective-permute-start | bytes 196616 | tf_op jit(solution)/shard_map/ppermute | solution.py:238
  23.0 3.5 %collective-permute-start.14 = (f32[128,128]{1,0:T(8,128)S(1)}, f32[128,128]{1,0:T(8,128)S(1)}, u32[]{:S(2)}, u32[]{:S(2)}) collective-permute-start(f32[128,128]{1,0:T(8,128)S(1)} %get-tuple-element.26), channel_id=1, source_target_pairs={{0,4},{4,0},{8,12},{12,8},{16,20},{20,16},{24,28},{28,24},{1,5},{5... | collective-permute-start | bytes 196616 | tf_op jit(solution)/shard_map/ppermute | solution.py:239
  23.0 9.5 %collective-permute-start.8 = (f32[128,256]{1,0:T(8,128)S(1)}, f32[128,256]{1,0:T(8,128)S(1)}, u32[]{:S(2)}, u32[]{:S(2)}) collective-permute-start(f32[128,256]{1,0:T(8,128)S(1)} %get-tuple-element.19), channel_id=1, source_target_pairs={{0,28},{4,8},{8,4},{12,16},{16,12},{20,24},{24,20},{28,0},{1,29},{... | collective-permute-start | bytes 393224 | tf_op jit(solution)/shard_map/ppermute | solution.py:238
  25.3 7.2 %collective-permute-start.9 = (f32[128,256]{1,0:T(8,128)S(1)}, f32[128,256]{1,0:T(8,128)S(1)}, u32[]{:S(2)}, u32[]{:S(2)}) collective-permute-start(f32[128,256]{1,0:T(8,128)S(1)} %get-tuple-element.20), channel_id=1, source_target_pairs={{0,4},{4,0},{8,12},{12,8},{16,20},{20,16},{24,28},{28,24},{1,5},{5... | collective-permute-start | bytes 393224 | tf_op jit(solution)/shard_map/ppermute | solution.py:239
  25.3 7.2 %collective-permute-start.12 = (f32[128,128]{1,0:T(8,128)S(1)}, f32[128,128]{1,0:T(8,128)S(1)}, u32[]{:S(2)}, u32[]{:S(2)}) collective-permute-start(f32[128,128]{1,0:T(8,128)S(1)} %add_add_fusion.1), channel_id=1, source_target_pairs={{0,1},{1,2},{2,3},{3,0},{4,5},{5,6},{6,7},{7,4},{8,9},{9,10},{10,1... | collective-permute-start | bytes 196616 | tf_op jit(solution)/shard_map/ppermute | solution.py:230
  26.5 6.0 %collective-permute-start.15 = (f32[128,128]{1,0:T(8,128)S(1)}, f32[128,128]{1,0:T(8,128)S(1)}, u32[]{:S(2)}, u32[]{:S(2)}) collective-permute-start(f32[128,128]{1,0:T(8,128)S(1)} %add_add_fusion), channel_id=1, source_target_pairs={{0,3},{1,0},{2,1},{3,2},{4,7},{5,4},{6,5},{7,6},{8,11},{9,8},{10,9... | collective-permute-start | bytes 196616 | tf_op jit(solution)/shard_map/ppermute | solution.py:230

commit v3 on v2

--- a/solution.py
+++ b/solution.py
@@ -74,11 +74,6 @@
 def by_table(values, high, low):
     first, second = split(values)
     return dot(first, high) + dot(second, high) + dot(first, low)
-
-
-def from_table(high, low, values):
-    first, second = split(values)
-    return dot(high, first) + dot(high, second) + dot(low, first)
 
 
 def spectrum_kernel(root_ref, mixed_ref, crossed_ref):
@@ -121,63 +116,39 @@
         crossed_ref[p * third:(p + 1) * third, :] = jnp.where(block_lane == 0, crossed * scale, 0.0)
 
 
-def swapped(odd, first, second):
-    return jnp.where(odd, second, first), jnp.where(odd, first, second)
-
-
-def filter_kernel(mid_far, mid_own, mid_near, left_far, left_own, left_near, right_far, right_own, right_near, mixed_ref,
-                  crossed_ref, row_ref, forward_ref, back_ref, mirror_ref, mid_far_out, mid_own_out, mid_near_out,
-                  left_far_out, left_own_out, left_near_out, right_far_out, right_own_out, right_near_out, real_ref, imag_ref,
-                  spec_ref):
-    third, half = mid_own.shape
-    quarter = half // 2
+def twice(block):
+    return jnp.concatenate([block, block], axis=0)
+
+
+def thirds(block):
+    third = block.shape[0] // 3
+    quarter = block.shape[1] // 2
+    return [
+        (block[j * third:(j + 1) * third, :quarter], block[j * third:(j + 1) * third, quarter:]) for j in range(3)
+    ]
+
+
+def spread(block):
+    (real_0, imag_0), (real_1, imag_1), (real_2, imag_2) = thirds(block)
     root_three = math.sqrt(3.0) / 2.0
-    odd_row = lax.axis_index("ty") % 2 == 1
-    mid_0, mid_2 = swapped(odd_row, mid_far[...], mid_near[...])
-    left_0, left_2 = swapped(odd_row, left_far[...], left_near[...])
-    right_0, right_2 = swapped(odd_row, right_far[...], right_near[...])
-    parts = ((mid_0, left_0, right_0), (mid_own[...], left_own[...], right_own[...]), (mid_2, left_2, right_2))
-    for j, (mid, left, right) in enumerate(parts):
-        first = mid[:, :quarter]
-        second = mid[:, quarter:]
-        even = jnp.concatenate([left + second, first + right], axis=1)
-        odd = jnp.concatenate([left - second, first - right], axis=1)
-        even = by_table(even, row_ref[0], row_ref[1])
-        odd = by_table(odd, row_ref[2], row_ref[3])
-        real_ref[j, :, :quarter] = even[:, :quarter]
-        real_ref[j, :, quarter:] = odd[:, :quarter]
-        imag_ref[j, :, :quarter] = even[:, quarter:]
-        imag_ref[j, :, quarter:] = odd[:, quarter:]
-    sum_real = real_ref[1] + real_ref[2]
-    sum_imag = imag_ref[1] + imag_ref[2]
-    gap_real = root_three * (real_ref[1] - real_ref[2])
-    gap_imag = root_three * (imag_ref[1] - imag_ref[2])
-    base_real = real_ref[0] - 0.5 * sum_real
-    base_imag = imag_ref[0] - 0.5 * sum_imag
-    inputs = (
-        (real_ref[0] + sum_real, imag_ref[0] + sum_imag),
-        (base_real + gap_imag, base_imag - gap_real),
-        (base_real - gap_imag, base_imag + gap_real),
-    )
-    for p, pair in enumerate(inputs):
-        stacked = jnp.concatenate(pair, axis=0)
-        spec_ref[p] = from_table(forward_ref[2 * p], forward_ref[2 * p + 1], stacked)
-    packed = []
-    for p in range(3):
-        high, low = split(spec_ref[(3 - p) % 3, :, :quarter])
-        flipped = dot(mirror_ref[min(p, 1)], jnp.concatenate([high, low], axis=1))
-        packed.append(flipped[:, :quarter] + flipped[:, quarter:])
-    outs = []
-    for p in range(3):
-        mixed = mixed_ref[p * third:(p + 1) * third, :]
-        mixed = jnp.concatenate([mixed, mixed], axis=0)
-        crossed = crossed_ref[p * third:(p + 1) * third, :]
-        crossed = jnp.concatenate([crossed, crossed], axis=0)
-        filtered = spec_ref[p] * mixed
-        filtered = jnp.concatenate([filtered[:, :quarter] + packed[p] * crossed, filtered[:, quarter:]], axis=1)
-        outs.append(from_table(back_ref[2 * p], back_ref[2 * p + 1], filtered))
-    real = [value[:third] for value in outs]
-    imag = [value[third:] for value in outs]
+    sum_real = real_1 + real_2
+    sum_imag = imag_1 + imag_2
+    gap_real = root_three * (real_1 - real_2)
+    gap_imag = root_three * (imag_1 - imag_2)
+    base_real = real_0 - 0.5 * sum_real
+    base_imag = imag_0 - 0.5 * sum_imag
+    return [
+        jnp.concatenate([real_0 + sum_real, imag_0 + sum_imag], axis=0),
+        jnp.concatenate([base_real + gap_imag, base_imag - gap_real], axis=0),
+        jnp.concatenate([base_real - gap_imag, base_imag + gap_real], axis=0),
+    ]
+
+
+def gathered(classes):
+    third = classes[0].shape[0] // 2
+    real = [value[:third] for value in classes]
+    imag = [value[third:] for value in classes]
+    root_three = math.sqrt(3.0) / 2.0
     sum_real = real[1] + real[2]
     sum_imag = imag[1] + imag[2]
     gap_real = root_three * (real[1] - real[2])
@@ -189,6 +160,83 @@
         (base_real - gap_imag, base_imag + gap_real),
         (base_real + gap_imag, base_imag - gap_real),
     )
+    return jnp.concatenate([jnp.concatenate(block, axis=1) for block in blocks], axis=0)
+
+
+def swapped(odd, first, second):
+    return jnp.where(odd, second, first), jnp.where(odd, first, second)
+
+
+def rows_kernel(mid_far, mid_own, mid_near, left_far, left_own, left_near, right_own, tables_ref, even_ref, odd_ref):
+    quarter = mid_own.shape[1] // 2
+    row_ref = tables_ref.at[:8]
+    odd_row = lax.axis_index("ty") % 2 == 1
+    mid_0, mid_2 = swapped(odd_row, mid_far[...], mid_near[...])
+    left_0, left_2 = swapped(odd_row, left_far[...], left_near[...])
+    evens = []
+    odds = []
+    for mid, left, right in ((mid_0, left_0, None), (mid_own[...], left_own[...], right_own[...]), (mid_2, left_2, None)):
+        first = mid[:, :quarter]
+        second = mid[:, quarter:]
+        plus, minus = (first, first) if right is None else (first + right, first - right)
+        evens.append(jnp.concatenate([left + second, plus], axis=1))
+        odds.append(jnp.concatenate([left - second, minus], axis=1))
+    even_ref[...] = by_table(jnp.concatenate(evens, axis=0), row_ref[0], row_ref[1])
+    odd_ref[...] = by_table(jnp.concatenate(odds, axis=0), row_ref[2], row_ref[3])
+
+
+def added(block, strips, high, low):
+    third = block.shape[0] // 3
+    quarter = strips[0].shape[1]
+    high = high[quarter:]
+    share = dot(jnp.concatenate(strips, axis=1), jnp.concatenate([high, high], axis=0)) + dot(strips[0], low[quarter:])
+    return jnp.concatenate([block[:third] + share[:third], block[third:2 * third], block[2 * third:] + share[third:]], axis=0)
+
+
+def filter_kernel(even_ref, odd_ref, right_far, right_near, mixed_ref, crossed_ref, tables_ref, mid_far_out, mid_own_out, mid_near_out, left_far_out, left_own_out, left_near_out,
+                  right_far_out, right_own_out, right_near_out):
+    third, half = mid_own_out.shape
+    row_ref, forward_ref, back_ref, mirror_ref = (tables_ref.at[a:b] for a, b in ((0, 8), (8, 14), (14, 20), (20, 22)))
+    quarter = half // 2
+    odd_row = lax.axis_index("ty") % 2 == 1
+    right = jnp.concatenate(swapped(odd_row, right_far[...], right_near[...]), axis=0)
+    even = added(even_ref[...], split(right), row_ref[0], row_ref[1])
+    odd = added(odd_ref[...], split(-right), row_ref[2], row_ref[3])
+    even_inputs = [split(value) for value in spread(even)]
+    even_main = [dot(forward_ref[2 * p], jnp.concatenate(even_inputs[p], axis=1)) for p in range(3)]
+    odd_inputs = [split(value) for value in spread(odd)]
+    even_spec = []
+    odd_spec = []
+    for p in range(3):
+        odd_main = dot(forward_ref[2 * p], jnp.concatenate(odd_inputs[p], axis=1))
+        rest = dot(forward_ref[2 * p + 1], jnp.concatenate([even_inputs[p][0], odd_inputs[p][0]], axis=1))
+        even_spec.append(even_main[p][:, :quarter] + even_main[p][:, quarter:] + rest[:, :quarter])
+        odd_spec.append(odd_main[:, :quarter] + odd_main[:, quarter:] + rest[:, quarter:])
+    even_parts = []
+    odd_parts = []
+    for p in range(3):
+        flipped = dot(mirror_ref[min(p, 1)], jnp.concatenate(split(even_spec[(3 - p) % 3]), axis=1))
+        flipped = flipped[:, :quarter] + flipped[:, quarter:]
+        rows = slice(p * third, (p + 1) * third)
+        even_gain = mixed_ref[rows, :quarter]
+        odd_gain = mixed_ref[rows, quarter:]
+        crossed = crossed_ref[rows, :]
+        filtered = even_spec[p] * twice(even_gain) + flipped * twice(crossed)
+        even_parts.append(split(filtered))
+        odd_parts.append(split(odd_spec[p] * twice(odd_gain)))
+    even_back = []
+    rests = []
+    for p in range(3):
+        main = dot(back_ref[2 * p], jnp.concatenate(even_parts[p], axis=1))
+        rest = dot(back_ref[2 * p + 1], jnp.concatenate([even_parts[p][0], odd_parts[p][0]], axis=1))
+        even_back.append(main[:, :quarter] + main[:, quarter:] + rest[:, :quarter])
+        rests.append(rest[:, quarter:])
+    odd_back = []
+    for p in range(3):
+        main = dot(back_ref[2 * p], jnp.concatenate(odd_parts[p], axis=1))
+        odd_back.append(main[:, :quarter] + main[:, quarter:] + rests[p])
+    even = by_table(gathered(even_back), row_ref[4], row_ref[5])
+    odd = by_table(gathered(odd_back), row_ref[6], row_ref[7])
     lane = lax.broadcasted_iota(jnp.int32, (1, half), 1).astype(F32)
     rising = (lane + 0.5) / half
     falling = 1.0 - rising
@@ -196,7 +244,7 @@
     mids = []
     lefts = []
     rights = []
-    for j, block in enumerate(blocks):
+    for j in range(3):
         knots = (row + 0.5) / third + j
         if j == 0:
             weight = 0.5 * knots * knots
@@ -204,12 +252,9 @@
             weight = 0.5 * (-2.0 * knots * knots + 6.0 * knots - 3.0)
         else:
             weight = 0.5 * (3.0 - knots) * (3.0 - knots)
-        even = jnp.concatenate([block[0][:, :quarter], block[1][:, :quarter]], axis=1)
-        odd = jnp.concatenate([block[0][:, quarter:], block[1][:, quarter:]], axis=1)
-        even = by_table(even, row_ref[4], row_ref[5])
-        odd = by_table(odd, row_ref[6], row_ref[7])
-        lower = (even + odd) * (weight * rising)
-        upper = (even - odd) * (weight * falling)
+        rows = slice(j * third, (j + 1) * third)
+        lower = (even[rows] + odd[rows]) * (weight * rising)
+        upper = (even[rows] - odd[rows]) * (weight * falling)
         lefts.append(lower[:, :quarter])
         rights.append(upper[:, quarter:])
         mids.append(jnp.concatenate([lower[:, quarter:], upper[:, :quarter]], axis=1))
@@ -243,9 +288,7 @@
 def per_device(noise, root_spectrum):
     margin, block_cols = noise.shape
     rows, cols = root_spectrum.shape
-    row_table = jnp.asarray(row_tables(cols))
-    forward_table, back_table = (jnp.asarray(t) for t in column_tables(rows))
-    mirror_table = jnp.asarray(mirror_tables(rows))
+    tables = jnp.asarray(np.concatenate([row_tables(cols), *column_tables(rows), mirror_tables(rows)]))
     limit = pltpu.CompilerParams(vmem_limit_bytes=24 * 1024 * 1024)
     mixed, crossed = pl.pallas_call(
         spectrum_kernel,
@@ -263,21 +306,25 @@
     right_far, right_near = exchanged(right, right, "ty")
     strip = jax.ShapeDtypeStruct((margin, margin), F32)
     block = jax.ShapeDtypeStruct((margin, block_cols), F32)
+    tall = jax.ShapeDtypeStruct((rows, block_cols), F32)
+    even, odd = pl.pallas_call(
+        rows_kernel,
+        out_shape=(tall, tall),
+        in_specs=whole(8),
+        out_specs=tuple(whole(2)),
+        compiler_params=limit,
+        cost_estimate=pl.CostEstimate(flops=10**7, bytes_accessed=10**4, transcendentals=0),
+        name="rows",
+    )(mid_far, noise, mid_near, left_far, left, left_near, right, tables)
     mid_far, mid, mid_near, left_far, left_own, left_near, right_far, right, right_near = pl.pallas_call(
         filter_kernel,
         out_shape=(block,) * 3 + (strip,) * 6,
-        in_specs=whole(15),
+        in_specs=whole(7),
         out_specs=tuple(whole(9)),
-        scratch_shapes=[
-            pltpu.VMEM((3, margin, block_cols), F32),
-            pltpu.VMEM((3, margin, block_cols), F32),
-            pltpu.VMEM((3, 2 * margin, block_cols), F32),
-        ],
         compiler_params=limit,
         cost_estimate=pl.CostEstimate(flops=4 * 10**9, bytes_accessed=10**7, transcendentals=0),
         name="filter",
-    )(mid_far, noise, mid_near, left_far, left, left_near, right_far, right, right_near, mixed, crossed,
-      row_table, forward_table, back_table, mirror_table)
+    )(even, odd, right_far, right_near, mixed, crossed, tables)
     right_far, right_near = exchanged(right_far, right_near, "ty")
     left_far, left_near = exchanged(left_far, left_near, "ty")
     mid_far, mid_near = exchanged(mid_far, mid_near, "ty")

time: 33.3 us -> 33.6 us (level)
  waiting for transfers between devices: 7.1 us -> 8.04 us
  starting transfers between devices: 19.4 us -> 18.8 us
    ppermute x4, starting transfers between devices: 9.29 us -> 8.02 us  [passed_along(): lax.ppermute(shard, axis, [(i, (i + by) % count) for i in range(count)])]
    ppermute x6, waiting for transfers between devices: 2.15 us -> 2.79 us  [exchanged(): from_far = lax.ppermute(to_far, axis, far)]
    ppermute x6, starting transfers between devices: 0.55 us -> 1.13 us  [exchanged(): from_near = lax.ppermute(to_near, axis, near)]
    pallas_call x0 -> x1, Pallas kernels: none -> 0.48 us  [per_device(): pl.pallas_call(rows_kernel, out_shape=(tall, tall), in_specs=whole(8), ou...]
    pallas_call x1, Pallas kernels: 2.32 us -> 1.84 us  [per_device(): pl.pallas_call(filter_kernel, out_shape=(block,) * 3 + (strip,) * 6, in_s...]
    unnamed x12 -> x6, local copies, waits for them, and re-layouts: 1.15 us -> 1.14 us
  transfers between devices with their start and end apart: 16 -> 16, of which waited for: 6 -> 6; matrix products, arithmetic and copies ran while one was open for 0% -> 0% of each run, Pallas kernels for 4% -> 6%
where the time goes in v3:
time: 33.6 us; the launch traced here: 33.4 us
  starting transfers between devices  18.8 us (56%)
  waiting for transfers between devices  8.04 us (24%)
  Pallas kernels  3.73 us (11%)
  local copies, waits for them, and re-layouts  2.02 us (6%)
  other arithmetic  0.72 us (2%)
    ppermute x6, starting transfers between devices, exchanged(): from_far = lax.ppermute(to_far, axis, far)  9.68 us
    ppermute x4, starting transfers between devices, passed_along(): lax.ppermute(shard, axis, [(i, (i + by) % count) for i in range(count)])  8.02 us
    ppermute x4, waiting for transfers between devices, passed_along(): lax.ppermute(shard, axis, [(i, (i + by) % count) for i in range(count)])  5.23 us
    ppermute x6, waiting for transfers between devices, exchanged(): from_far = lax.ppermute(to_far, axis, far)  2.79 us
    pallas_call x1, Pallas kernels, per_device(): pl.pallas_call(filter_kernel, out_shape=(block,) * 3 + (strip,) * 6, in_s...  1.84 us
    pallas_call x1, Pallas kernels, per_device(): pl.pallas_call(spectrum_kernel, out_shape=(jax.ShapeDtypeStruct((rows, co...  1.41 us
    unnamed x6, local copies, waits for them, and re-layouts  1.14 us
    ppermute x6, starting transfers between devices, exchanged(): from_near = lax.ppermute(to_near, axis, near)  1.13 us
  transfers between devices with their start and end apart: 16, of which 6 were waited for; matrix products, arithmetic and copies ran while one was open for 0% of the time, Pallas kernels for 6%

profile of v3, /device:TPU:0, one launch (start us, length us, event | category | flops | bytes accessed | tf_op | source)
XLA Modules:
  0.0 33.4 jit_solution(571926349893113296)
XLA Ops:
  0.0 0.9 %fusion = (f32[128,128]{1,0:T(8,128)S(1)}, f32[128,128]{1,0:T(8,128)S(1)}) fusion(f32[128,256]{1,0:T(8,128)} %mid_own.1), kind=kLoop, calls=%fused_computation.3 | loop fusion | bytes 262144 | tf_op jit(solution)/shard_map/slice | solution.py:303
  0.9 3.1 %collective-permute-start.2 = (f32[128,128]{1,0:T(8,128)S(1)}, f32[128,128]{1,0:T(8,128)S(1)}, u32[]{:S(2)}, u32[]{:S(2)}) collective-permute-start(f32[128,128]{1,0:T(8,128)S(1)} %get-tuple-element.32), channel_id=1, source_target_pairs={{0,1},{1,2},{2,3},{3,0},{4,5},{5,6},{6,7},{7,4},{8,9},{9,10},{10,1... | collective-permute-start | bytes 196616 | tf_op jit(solution)/shard_map/ppermute | solution.py:275
  4.0 2.1 %collective-permute-start.5 = (f32[128,128]{1,0:T(8,128)S(1)}, f32[128,128]{1,0:T(8,128)S(1)}, u32[]{:S(2)}, u32[]{:S(2)}) collective-permute-start(f32[128,128]{1,0:T(8,128)S(1)} %get-tuple-element.31), channel_id=1, source_target_pairs={{0,3},{1,0},{2,1},{3,2},{4,7},{5,4},{6,5},{7,6},{8,11},{9,8},{10,9... | collective-permute-start | bytes 196616 | tf_op jit(solution)/shard_map/ppermute | solution.py:275
  6.1 2.2 %collective-permute-done.2.left_own = f32[128,128]{1,0:T(8,128)S(1)} collective-permute-done((f32[128,128]{1,0:T(8,128)S(1)}, f32[128,128]{1,0:T(8,128)S(1)}, u32[]{:S(2)}, u32[]{:S(2)}) %collective-permute-start.2) | collective-permute-done | bytes 65568 | tf_op jit(solution)/shard_map/ppermute | solution.py:275
  8.4 0.5 %collective-permute-start.1 = (f32[128,256]{1,0:T(8,128)}, f32[128,256]{1,0:T(8,128)S(1)}, u32[]{:S(2)}, u32[]{:S(2)}) collective-permute-start(f32[128,256]{1,0:T(8,128)} %mid_own.1), channel_id=1, source_target_pairs={{0,4},{4,0},{8,12},{12,8},{16,20},{20,16},{24,28},{28,24},{1,5},{5... | collective-permute-start | bytes 393224 | tf_op jit(solution)/shard_map/ppermute | solution.py:284
  8.9 2.5 %collective-permute-start = (f32[128,256]{1,0:T(8,128)}, f32[128,256]{1,0:T(8,128)S(1)}, u32[]{:S(2)}, u32[]{:S(2)}) collective-permute-start(f32[128,256]{1,0:T(8,128)} %mid_own.1), channel_id=1, source_target_pairs={{0,28},{4,8},{8,4},{12,16},{16,12},{20,24},{24,20},{28,0},{1,29},{... | collective-permute-start | bytes 393224 | tf_op jit(solution)/shard_map/ppermute | solution.py:283
  11.4 0.6 %collective-permute-start.6 = (f32[128,128]{1,0:T(8,128)S(1)}, f32[128,128]{1,0:T(8,128)S(1)}, u32[]{:S(2)}, u32[]{:S(2)}) collective-permute-start(f32[128,128]{1,0:T(8,128)S(1)} %collective-permute-done.5.right_own), channel_id=1, source_target_pairs={{0,28},{4,8},{8,4},{12,16},{16,12},{20,24},{24,20},{28,0},{1,29},{... | collective-permute-start | bytes 196616 | tf_op jit(solution)/shard_map/ppermute | solution.py:283
  12.0 2.0 %collective-permute-start.3 = (f32[128,128]{1,0:T(8,128)S(1)}, f32[128,128]{1,0:T(8,128)S(1)}, u32[]{:S(2)}, u32[]{:S(2)}) collective-permute-start(f32[128,128]{1,0:T(8,128)S(1)} %collective-permute-done.2.left_own), channel_id=1, source_target_pairs={{0,28},{4,8},{8,4},{12,16},{16,12},{20,24},{24,20},{28,0},{1,29},{... | collective-permute-start | bytes 196616 | tf_op jit(solution)/shard_map/ppermute | solution.py:283
  14.0 1.1 %copy-done.2 = f32[384,512]{1,0:T(8,128)S(1)} copy-done((f32[384,512]{1,0:T(8,128)S(1)}, f32[384,512]{1,0:T(8,128)}, u32[]{:S(2)}) %copy-start.2) | copy-done | bytes 786456
  15.1 1.4 %spectrum.1 = (f32[384,256]{1,0:T(8,128)S(1)}, f32[384,128]{1,0:T(8,128)S(1)}) custom-call(f32[384,512]{1,0:T(8,128)S(1)} %copy-done.2), custom_call_target="tpu_custom_call" | custom-call | flops 2000000000 | bytes 1000000 | tf_op jit(solution)/shard_map/spectrum/pallas_call | solution.py:293
  16.6 1.5 %collective-permute-done.3.left_far = f32[128,128]{1,0:T(8,128)S(1)} collective-permute-done((f32[128,128]{1,0:T(8,128)S(1)}, f32[128,128]{1,0:T(8,128)S(1)}, u32[]{:S(2)}, u32[]{:S(2)}) %collective-permute-start.3) | collective-permute-done | bytes 65568 | tf_op jit(solution)/shard_map/ppermute | solution.py:283
  18.1 0.5 %rows.1 = (f32[384,256]{1,0:T(8,128)S(1)}, f32[384,256]{1,0:T(8,128)S(1)}) custom-call(f32[128,256]{1,0:T(8,128)S(1)} %collective-permute-done.mid_far, f32[128,256]{1,0:T(8,128)S(1)} %copy-done.1, f32[128,256]{1,0:T(8,128)S(1)} %collective-permute-done.1.mid_near, f32[128,128]{1,0:T(8,128)S(1)} %collective-permute-done.3.left_far, ...), custom_call_target="tpu_custom_call" | custom-call | flops 10000000 | bytes 10000 | tf_op jit(solution)/shard_map/rows/pallas_call | solution.py:310
  18.6 1.8 %filter.1 = (f32[128,256]{1,0:T(8,128)S(1)}, f32[128,256]{1,0:T(8,128)S(1)}, f32[128,256]{1,0:T(8,128)S(1)}, f32[128,128]{1,0:T(8,128)S(1)}, f32[128,128]{1,0:T(...) custom-call(f32[384,256]{1,0:T(8,128)S(1)} %get-tuple-element.18.eve, ...), custom_call_target="tpu_custom_call" | custom-call | flops 4000000000 | bytes 10000000 | tf_op jit(solution)/shard_map/filter/pallas_call | solution.py:319
  20.4 1.9 %collective-permute-start.10 = (f32[128,128]{1,0:T(8,128)S(1)}, f32[128,128]{1,0:T(8,128)S(1)}, u32[]{:S(2)}, u32[]{:S(2)}) collective-permute-start(f32[128,128]{1,0:T(8,128)S(1)} %get-tuple-element.26), channel_id=1, source_target_pairs={{0,28},{4,8},{8,4},{12,16},{16,12},{20,24},{24,20},{28,0},{1,29},{... | collective-permute-start | bytes 196616 | tf_op jit(solution)/shard_map/ppermute | solution.py:283
  22.4 0.8 %collective-permute-start.13 = (f32[128,128]{1,0:T(8,128)S(1)}, f32[128,128]{1,0:T(8,128)S(1)}, u32[]{:S(2)}, u32[]{:S(2)}) collective-permute-start(f32[128,128]{1,0:T(8,128)S(1)} %get-tuple-element.29), channel_id=1, source_target_pairs={{0,28},{4,8},{8,4},{12,16},{16,12},{20,24},{24,20},{28,0},{1,29},{... | collective-permute-start | bytes 196616 | tf_op jit(solution)/shard_map/ppermute | solution.py:283
  23.2 0.6 %collective-permute-start.14 = (f32[128,128]{1,0:T(8,128)S(1)}, f32[128,128]{1,0:T(8,128)S(1)}, u32[]{:S(2)}, u32[]{:S(2)}) collective-permute-start(f32[128,128]{1,0:T(8,128)S(1)} %get-tuple-element.30), channel_id=1, source_target_pairs={{0,4},{4,0},{8,12},{12,8},{16,20},{20,16},{24,28},{28,24},{1,5},{5... | collective-permute-start | bytes 196616 | tf_op jit(solution)/shard_map/ppermute | solution.py:284
  23.8 1.8 %collective-permute-start.8 = (f32[128,256]{1,0:T(8,128)S(1)}, f32[128,256]{1,0:T(8,128)S(1)}, u32[]{:S(2)}, u32[]{:S(2)}) collective-permute-start(f32[128,256]{1,0:T(8,128)S(1)} %get-tuple-element.23), channel_id=1, source_target_pairs={{0,28},{4,8},{8,4},{12,16},{16,12},{20,24},{24,20},{28,0},{1,29},{... | collective-permute-start | bytes 393224 | tf_op jit(solution)/shard_map/ppermute | solution.py:283
  25.6 0.2 collective-permute-done.10
  25.8 0.1 collective-permute-start.12
  25.9 1.1 %collective-permute-done.13 = f32[128,128]{1,0:T(8,128)S(1)} collective-permute-done((f32[128,128]{1,0:T(8,128)S(1)}, f32[128,128]{1,0:T(8,128)S(1)}, u32[]{:S(2)}, u32[]{:S(2)}) %collective-permute-start.13) | collective-permute-done | bytes 65568 | tf_op jit(solution)/shard_map/ppermute | solution.py:283
  27.0 2.7 %collective-permute-start.15 = (f32[128,128]{1,0:T(8,128)S(1)}, f32[128,128]{1,0:T(8,128)S(1)}, u32[]{:S(2)}, u32[]{:S(2)}) collective-permute-start(f32[128,128]{1,0:T(8,128)S(1)} %add_add_fusion), channel_id=1, source_target_pairs={{0,3},{1,0},{2,1},{3,2},{4,7},{5,4},{6,5},{7,6},{8,11},{9,8},{10,9... | collective-permute-start | bytes 196616 | tf_op jit(solution)/shard_map/ppermute | solution.py:275
  29.7 2.9 %collective-permute-done.12 = f32[128,128]{1,0:T(8,128)S(1)} collective-permute-done((f32[128,128]{1,0:T(8,128)S(1)}, f32[128,128]{1,0:T(8,128)S(1)}, u32[]{:S(2)}, u32[]{:S(2)}) %collective-permute-start.12) | collective-permute-done | bytes 65568 | tf_op jit(solution)/shard_map/ppermute | solution.py:275
  32.6 0.1 collective-permute-done.15
  32.7 0.7 %maximum_add_fusion = f32[128,256]{1,0:T(8,128)} fusion(f32[128,128]{1,0:T(8,128)S(1)} %collective-permute-done.15, f32[128,128]{1,0:T(8,128)S(1)} %collective-permute-done.12, f32[128,256]{1,0:T(8,128)S(1)} %collective-permute-done.9, f32[128,256]{1,0:T(8,128)S(1)} %get-tuple-element.22, f32[128,256]{1,0:T(8,128)S(1)} %collective-permute-done.8), kind=kLoop, calls=%fused_computation | loop fusion | flops 131072 | bytes 655360 | tf_op jit(solution)/shard_map/add | solution.py:334
  (21 shorter events, 0.1 us)
Async XLA Ops:
  0.9 7.5 %collective-permute-start.2 = (f32[128,128]{1,0:T(8,128)S(1)}, f32[128,128]{1,0:T(8,128)S(1)}, u32[]{:S(2)}, u32[]{:S(2)}) collective-permute-start(f32[128,128]{1,0:T(8,128)S(1)} %get-tuple-element.32), channel_id=1, source_target_pairs={{0,1},{1,2},{2,3},{3,0},{4,5},{5,6},{6,7},{7,4},{8,9},{9,10},{10,1... | collective-permute-start | bytes 196616 | tf_op jit(solution)/shard_map/ppermute | solution.py:275
  4.0 14.1 %copy-start = (bf16[22,256,256]{2,1,0:T(8,128)(2,1)S(1)}, bf16[22,256,256]{2,1,0:T(8,128)(2,1)}, u32[]{:S(2)}) copy-start(bf16[22,256,256]{2,1,0:T(8,128)(2,1)} %constant.2.clone.tables_ref) | copy-start | bytes 8650756
  4.0 14.1 %copy-start.1 = (f32[128,256]{1,0:T(8,128)S(1)}, f32[128,256]{1,0:T(8,128)}, u32[]{:S(2)}) copy-start(f32[128,256]{1,0:T(8,128)} %mid_own.1) | copy-start | bytes 393220
  4.0 7.4 %collective-permute-start.5 = (f32[128,128]{1,0:T(8,128)S(1)}, f32[128,128]{1,0:T(8,128)S(1)}, u32[]{:S(2)}, u32[]{:S(2)}) collective-permute-start(f32[128,128]{1,0:T(8,128)S(1)} %get-tuple-element.31), channel_id=1, source_target_pairs={{0,3},{1,0},{2,1},{3,2},{4,7},{5,4},{6,5},{7,6},{8,11},{9,8},{10,9... | collective-permute-start | bytes 196616 | tf_op jit(solution)/shard_map/ppermute | solution.py:275
  8.4 3.7 %collective-permute-start.4 = (f32[128,128]{1,0:T(8,128)S(1)}, f32[128,128]{1,0:T(8,128)S(1)}, u32[]{:S(2)}, u32[]{:S(2)}) collective-permute-start(f32[128,128]{1,0:T(8,128)S(1)} %collective-permute-done.2.left_own), channel_id=1, source_target_pairs={{0,4},{4,0},{8,12},{12,8},{16,20},{20,16},{24,28},{28,24},{1,5},{5... | collective-permute-start | bytes 196616 | tf_op jit(solution)/shard_map/ppermute | solution.py:284
  8.4 9.7 %collective-permute-start.1 = (f32[128,256]{1,0:T(8,128)}, f32[128,256]{1,0:T(8,128)S(1)}, u32[]{:S(2)}, u32[]{:S(2)}) collective-permute-start(f32[128,256]{1,0:T(8,128)} %mid_own.1), channel_id=1, source_target_pairs={{0,4},{4,0},{8,12},{12,8},{16,20},{20,16},{24,28},{28,24},{1,5},{5... | collective-permute-start | bytes 393224 | tf_op jit(solution)/shard_map/ppermute | solution.py:284
  8.9 9.2 %collective-permute-start = (f32[128,256]{1,0:T(8,128)}, f32[128,256]{1,0:T(8,128)S(1)}, u32[]{:S(2)}, u32[]{:S(2)}) collective-permute-start(f32[128,256]{1,0:T(8,128)} %mid_own.1), channel_id=1, source_target_pairs={{0,28},{4,8},{8,4},{12,16},{16,12},{20,24},{24,20},{28,0},{1,29},{... | collective-permute-start | bytes 393224 | tf_op jit(solution)/shard_map/ppermute | solution.py:283
  11.4 7.2 %collective-permute-start.7 = (f32[128,128]{1,0:T(8,128)S(1)}, f32[128,128]{1,0:T(8,128)S(1)}, u32[]{:S(2)}, u32[]{:S(2)}) collective-permute-start(f32[128,128]{1,0:T(8,128)S(1)} %collective-permute-done.5.right_own), channel_id=1, source_target_pairs={{0,4},{4,0},{8,12},{12,8},{16,20},{20,16},{24,28},{28,24},{1,5},{5... | collective-permute-start | bytes 196616 | tf_op jit(solution)/shard_map/ppermute | solution.py:284
  11.4 7.2 %collective-permute-start.6 = (f32[128,128]{1,0:T(8,128)S(1)}, f32[128,128]{1,0:T(8,128)S(1)}, u32[]{:S(2)}, u32[]{:S(2)}) collective-permute-start(f32[128,128]{1,0:T(8,128)S(1)} %collective-permute-done.5.right_own), channel_id=1, source_target_pairs={{0,28},{4,8},{8,4},{12,16},{16,12},{20,24},{24,20},{28,0},{1,29},{... | collective-permute-start | bytes 196616 | tf_op jit(solution)/shard_map/ppermute | solution.py:283
  12.0 6.0 %collective-permute-start.3 = (f32[128,128]{1,0:T(8,128)S(1)}, f32[128,128]{1,0:T(8,128)S(1)}, u32[]{:S(2)}, u32[]{:S(2)}) collective-permute-start(f32[128,128]{1,0:T(8,128)S(1)} %collective-permute-done.2.left_own), channel_id=1, source_target_pairs={{0,28},{4,8},{8,4},{12,16},{16,12},{20,24},{24,20},{28,0},{1,29},{... | collective-permute-start | bytes 196616 | tf_op jit(solution)/shard_map/ppermute | solution.py:283
  14.0 1.1 %copy-start.2 = (f32[384,512]{1,0:T(8,128)S(1)}, f32[384,512]{1,0:T(8,128)}, u32[]{:S(2)}) copy-start(f32[384,512]{1,0:T(8,128)} %root_ref.1) | copy-start | bytes 2359300
  20.4 5.3 %collective-permute-start.10 = (f32[128,128]{1,0:T(8,128)S(1)}, f32[128,128]{1,0:T(8,128)S(1)}, u32[]{:S(2)}, u32[]{:S(2)}) collective-permute-start(f32[128,128]{1,0:T(8,128)S(1)} %get-tuple-element.26), channel_id=1, source_target_pairs={{0,28},{4,8},{8,4},{12,16},{16,12},{20,24},{24,20},{28,0},{1,29},{... | collective-permute-start | bytes 196616 | tf_op jit(solution)/shard_map/ppermute | solution.py:283
  22.4 3.4 %collective-permute-start.11 = (f32[128,128]{1,0:T(8,128)S(1)}, f32[128,128]{1,0:T(8,128)S(1)}, u32[]{:S(2)}, u32[]{:S(2)}) collective-permute-start(f32[128,128]{1,0:T(8,128)S(1)} %get-tuple-element.27), channel_id=1, source_target_pairs={{0,4},{4,0},{8,12},{12,8},{16,20},{20,16},{24,28},{28,24},{1,5},{5... | collective-permute-start | bytes 196616 | tf_op jit(solution)/shard_map/ppermute | solution.py:284
  22.4 4.6 %collective-permute-start.13 = (f32[128,128]{1,0:T(8,128)S(1)}, f32[128,128]{1,0:T(8,128)S(1)}, u32[]{:S(2)}, u32[]{:S(2)}) collective-permute-start(f32[128,128]{1,0:T(8,128)S(1)} %get-tuple-element.29), channel_id=1, source_target_pairs={{0,28},{4,8},{8,4},{12,16},{16,12},{20,24},{24,20},{28,0},{1,29},{... | collective-permute-start | bytes 196616 | tf_op jit(solution)/shard_map/ppermute | solution.py:283
  23.2 3.8 %collective-permute-start.14 = (f32[128,128]{1,0:T(8,128)S(1)}, f32[128,128]{1,0:T(8,128)S(1)}, u32[]{:S(2)}, u32[]{:S(2)}) collective-permute-start(f32[128,128]{1,0:T(8,128)S(1)} %get-tuple-element.30), channel_id=1, source_target_pairs={{0,4},{4,0},{8,12},{12,8},{16,20},{20,16},{24,28},{28,24},{1,5},{5... | collective-permute-start | bytes 196616 | tf_op jit(solution)/shard_map/ppermute | solution.py:284
  23.8 9.0 %collective-permute-start.8 = (f32[128,256]{1,0:T(8,128)S(1)}, f32[128,256]{1,0:T(8,128)S(1)}, u32[]{:S(2)}, u32[]{:S(2)}) collective-permute-start(f32[128,256]{1,0:T(8,128)S(1)} %get-tuple-element.23), channel_id=1, source_target_pairs={{0,28},{4,8},{8,4},{12,16},{16,12},{20,24},{24,20},{28,0},{1,29},{... | collective-permute-start | bytes 393224 | tf_op jit(solution)/shard_map/ppermute | solution.py:283
  25.8 7.0 %collective-permute-start.9 = (f32[128,256]{1,0:T(8,128)S(1)}, f32[128,256]{1,0:T(8,128)S(1)}, u32[]{:S(2)}, u32[]{:S(2)}) collective-permute-start(f32[128,256]{1,0:T(8,128)S(1)} %get-tuple-element.24), channel_id=1, source_target_pairs={{0,4},{4,0},{8,12},{12,8},{16,20},{20,16},{24,28},{28,24},{1,5},{5... | collective-permute-start | bytes 393224 | tf_op jit(solution)/shard_map/ppermute | solution.py:284
  25.8 6.8 %collective-permute-start.12 = (f32[128,128]{1,0:T(8,128)S(1)}, f32[128,128]{1,0:T(8,128)S(1)}, u32[]{:S(2)}, u32[]{:S(2)}) collective-permute-start(f32[128,128]{1,0:T(8,128)S(1)} %add_add_fusion.1), channel_id=1, source_target_pairs={{0,1},{1,2},{2,3},{3,0},{4,5},{5,6},{6,7},{7,4},{8,9},{9,10},{10,1... | collective-permute-start | bytes 196616 | tf_op jit(solution)/shard_map/ppermute | solution.py:275
  27.0 5.7 %collective-permute-start.15 = (f32[128,128]{1,0:T(8,128)S(1)}, f32[128,128]{1,0:T(8,128)S(1)}, u32[]{:S(2)}, u32[]{:S(2)}) collective-permute-start(f32[128,128]{1,0:T(8,128)S(1)} %add_add_fusion), channel_id=1, source_target_pairs={{0,3},{1,0},{2,1},{3,2},{4,7},{5,4},{6,5},{7,6},{8,11},{9,8},{10,9... | collective-permute-start | bytes 196616 | tf_op jit(solution)/shard_map/ppermute | solution.py:275

commit v4 on v3

--- a/solution.py
+++ b/solution.py
@@ -212,31 +212,29 @@
         rest = dot(forward_ref[2 * p + 1], jnp.concatenate([even_inputs[p][0], odd_inputs[p][0]], axis=1))
         even_spec.append(even_main[p][:, :quarter] + even_main[p][:, quarter:] + rest[:, :quarter])
         odd_spec.append(odd_main[:, :quarter] + odd_main[:, quarter:] + rest[:, quarter:])
+    odd_parts = []
+    for p in range(3):
+        odd_parts.append(split(odd_spec[p] * twice(mixed_ref[p * third:(p + 1) * third, quarter:])))
     even_parts = []
-    odd_parts = []
     for p in range(3):
         flipped = dot(mirror_ref[min(p, 1)], jnp.concatenate(split(even_spec[(3 - p) % 3]), axis=1))
         flipped = flipped[:, :quarter] + flipped[:, quarter:]
         rows = slice(p * third, (p + 1) * third)
-        even_gain = mixed_ref[rows, :quarter]
-        odd_gain = mixed_ref[rows, quarter:]
-        crossed = crossed_ref[rows, :]
-        filtered = even_spec[p] * twice(even_gain) + flipped * twice(crossed)
+        filtered = even_spec[p] * twice(mixed_ref[rows, :quarter]) + flipped * twice(crossed_ref[rows, :])
         even_parts.append(split(filtered))
-        odd_parts.append(split(odd_spec[p] * twice(odd_gain)))
+    odd_main = [dot(back_ref[2 * p], jnp.concatenate(odd_parts[p], axis=1)) for p in range(3)]
+    odd_back = []
+    rests = []
+    for p in range(3):
+        rest = dot(back_ref[2 * p + 1], jnp.concatenate([even_parts[p][0], odd_parts[p][0]], axis=1))
+        odd_back.append(odd_main[p][:, :quarter] + odd_main[p][:, quarter:] + rest[:, quarter:])
+        rests.append(rest[:, :quarter])
     even_back = []
-    rests = []
     for p in range(3):
         main = dot(back_ref[2 * p], jnp.concatenate(even_parts[p], axis=1))
-        rest = dot(back_ref[2 * p + 1], jnp.concatenate([even_parts[p][0], odd_parts[p][0]], axis=1))
-        even_back.append(main[:, :quarter] + main[:, quarter:] + rest[:, :quarter])
-        rests.append(rest[:, quarter:])
-    odd_back = []
-    for p in range(3):
-        main = dot(back_ref[2 * p], jnp.concatenate(odd_parts[p], axis=1))
-        odd_back.append(main[:, :quarter] + main[:, quarter:] + rests[p])
+        even_back.append(main[:, :quarter] + main[:, quarter:] + rests[p])
+    odd = by_table(gathered(odd_back), row_ref[6], row_ref[7])
     even = by_table(gathered(even_back), row_ref[4], row_ref[5])
-    odd = by_table(gathered(odd_back), row_ref[6], row_ref[7])
     lane = lax.broadcasted_iota(jnp.int32, (1, half), 1).astype(F32)
     rising = (lane + 0.5) / half
     falling = 1.0 - rising

time: 33.6 us -> 33.5 us (level)
  no operation moved by 1% of the time
where the time goes in v4:
time: 33.5 us; the launch traced here: 33.3 us
  starting transfers between devices  18.8 us (56%)
  waiting for transfers between devices  8.04 us (24%)
  Pallas kernels  3.66 us (11%)
  local copies, waits for them, and re-layouts  2.02 us (6%)
  other arithmetic  0.72 us (2%)
    ppermute x6, starting transfers between devices, exchanged(): from_far = lax.ppermute(to_far, axis, far)  9.68 us
    ppermute x4, starting transfers between devices, passed_along(): lax.ppermute(shard, axis, [(i, (i + by) % count) for i in range(count)])  8.02 us
    ppermute x4, waiting for transfers between devices, passed_along(): lax.ppermute(shard, axis, [(i, (i + by) % count) for i in range(count)])  5.23 us
    ppermute x6, waiting for transfers between devices, exchanged(): from_far = lax.ppermute(to_far, axis, far)  2.79 us
    pallas_call x1, Pallas kernels, per_device(): pl.pallas_call(filter_kernel, out_shape=(block,) * 3 + (strip,) * 6, in_s...  1.77 us
    pallas_call x1, Pallas kernels, per_device(): pl.pallas_call(spectrum_kernel, out_shape=(jax.ShapeDtypeStruct((rows, co...  1.41 us
    unnamed x6, local copies, waits for them, and re-layouts  1.14 us
    ppermute x6, starting transfers between devices, exchanged(): from_near = lax.ppermute(to_near, axis, near)  1.13 us
  transfers between devices with their start and end apart: 16, of which 6 were waited for; matrix products, arithmetic and copies ran while one was open for 0% of the time, Pallas kernels for 6%

profile of v4, /device:TPU:0, one launch (start us, length us, event | category | flops | bytes accessed | tf_op | source)
XLA Modules:
  0.0 33.3 jit_solution(9483829049949209961)
XLA Ops:
  0.0 0.9 %fusion = (f32[128,128]{1,0:T(8,128)S(1)}, f32[128,128]{1,0:T(8,128)S(1)}) fusion(f32[128,256]{1,0:T(8,128)} %mid_own.1), kind=kLoop, calls=%fused_computation.3 | loop fusion | bytes 262144 | tf_op jit(solution)/shard_map/slice | solution.py:301
  0.9 3.1 %collective-permute-start.2 = (f32[128,128]{1,0:T(8,128)S(1)}, f32[128,128]{1,0:T(8,128)S(1)}, u32[]{:S(2)}, u32[]{:S(2)}) collective-permute-start(f32[128,128]{1,0:T(8,128)S(1)} %get-tuple-element.32), channel_id=1, source_target_pairs={{0,1},{1,2},{2,3},{3,0},{4,5},{5,6},{6,7},{7,4},{8,9},{9,10},{10,1... | collective-permute-start | bytes 196616 | tf_op jit(solution)/shard_map/ppermute | solution.py:273
  4.0 2.1 %collective-permute-start.5 = (f32[128,128]{1,0:T(8,128)S(1)}, f32[128,128]{1,0:T(8,128)S(1)}, u32[]{:S(2)}, u32[]{:S(2)}) collective-permute-start(f32[128,128]{1,0:T(8,128)S(1)} %get-tuple-element.31), channel_id=1, source_target_pairs={{0,3},{1,0},{2,1},{3,2},{4,7},{5,4},{6,5},{7,6},{8,11},{9,8},{10,9... | collective-permute-start | bytes 196616 | tf_op jit(solution)/shard_map/ppermute | solution.py:273
  6.1 2.2 %collective-permute-done.2.left_own = f32[128,128]{1,0:T(8,128)S(1)} collective-permute-done((f32[128,128]{1,0:T(8,128)S(1)}, f32[128,128]{1,0:T(8,128)S(1)}, u32[]{:S(2)}, u32[]{:S(2)}) %collective-permute-start.2) | collective-permute-done | bytes 65568 | tf_op jit(solution)/shard_map/ppermute | solution.py:273
  8.4 0.5 %collective-permute-start.1 = (f32[128,256]{1,0:T(8,128)}, f32[128,256]{1,0:T(8,128)S(1)}, u32[]{:S(2)}, u32[]{:S(2)}) collective-permute-start(f32[128,256]{1,0:T(8,128)} %mid_own.1), channel_id=1, source_target_pairs={{0,4},{4,0},{8,12},{12,8},{16,20},{20,16},{24,28},{28,24},{1,5},{5... | collective-permute-start | bytes 393224 | tf_op jit(solution)/shard_map/ppermute | solution.py:282
  8.9 2.5 %collective-permute-start = (f32[128,256]{1,0:T(8,128)}, f32[128,256]{1,0:T(8,128)S(1)}, u32[]{:S(2)}, u32[]{:S(2)}) collective-permute-start(f32[128,256]{1,0:T(8,128)} %mid_own.1), channel_id=1, source_target_pairs={{0,28},{4,8},{8,4},{12,16},{16,12},{20,24},{24,20},{28,0},{1,29},{... | collective-permute-start | bytes 393224 | tf_op jit(solution)/shard_map/ppermute | solution.py:281
  11.4 0.6 %collective-permute-start.6 = (f32[128,128]{1,0:T(8,128)S(1)}, f32[128,128]{1,0:T(8,128)S(1)}, u32[]{:S(2)}, u32[]{:S(2)}) collective-permute-start(f32[128,128]{1,0:T(8,128)S(1)} %collective-permute-done.5.right_own), channel_id=1, source_target_pairs={{0,28},{4,8},{8,4},{12,16},{16,12},{20,24},{24,20},{28,0},{1,29},{... | collective-permute-start | bytes 196616 | tf_op jit(solution)/shard_map/ppermute | solution.py:281
  12.0 2.0 %collective-permute-start.3 = (f32[128,128]{1,0:T(8,128)S(1)}, f32[128,128]{1,0:T(8,128)S(1)}, u32[]{:S(2)}, u32[]{:S(2)}) collective-permute-start(f32[128,128]{1,0:T(8,128)S(1)} %collective-permute-done.2.left_own), channel_id=1, source_target_pairs={{0,28},{4,8},{8,4},{12,16},{16,12},{20,24},{24,20},{28,0},{1,29},{... | collective-permute-start | bytes 196616 | tf_op jit(solution)/shard_map/ppermute | solution.py:281
  14.0 1.1 %copy-done.2 = f32[384,512]{1,0:T(8,128)S(1)} copy-done((f32[384,512]{1,0:T(8,128)S(1)}, f32[384,512]{1,0:T(8,128)}, u32[]{:S(2)}) %copy-start.2) | copy-done | bytes 786456
  15.1 1.4 %spectrum.1 = (f32[384,256]{1,0:T(8,128)S(1)}, f32[384,128]{1,0:T(8,128)S(1)}) custom-call(f32[384,512]{1,0:T(8,128)S(1)} %copy-done.2), custom_call_target="tpu_custom_call" | custom-call | flops 2000000000 | bytes 1000000 | tf_op jit(solution)/shard_map/spectrum/pallas_call | solution.py:291
  16.6 1.5 %collective-permute-done.3.left_far = f32[128,128]{1,0:T(8,128)S(1)} collective-permute-done((f32[128,128]{1,0:T(8,128)S(1)}, f32[128,128]{1,0:T(8,128)S(1)}, u32[]{:S(2)}, u32[]{:S(2)}) %collective-permute-start.3) | collective-permute-done | bytes 65568 | tf_op jit(solution)/shard_map/ppermute | solution.py:281
  18.1 0.5 %rows.1 = (f32[384,256]{1,0:T(8,128)S(1)}, f32[384,256]{1,0:T(8,128)S(1)}) custom-call(f32[128,256]{1,0:T(8,128)S(1)} %collective-permute-done.mid_far, f32[128,256]{1,0:T(8,128)S(1)} %copy-done.1, f32[128,256]{1,0:T(8,128)S(1)} %collective-permute-done.1.mid_near, f32[128,128]{1,0:T(8,128)S(1)} %collective-permute-done.3.left_far, ...), custom_call_target="tpu_custom_call" | custom-call | flops 10000000 | bytes 10000 | tf_op jit(solution)/shard_map/rows/pallas_call | solution.py:308
  18.6 1.8 %filter.1 = (f32[128,256]{1,0:T(8,128)S(1)}, f32[128,256]{1,0:T(8,128)S(1)}, f32[128,256]{1,0:T(8,128)S(1)}, f32[128,128]{1,0:T(8,128)S(1)}, f32[128,128]{1,0:T(...) custom-call(f32[384,256]{1,0:T(8,128)S(1)} %get-tuple-element.18.eve, ...), custom_call_target="tpu_custom_call" | custom-call | flops 4000000000 | bytes 10000000 | tf_op jit(solution)/shard_map/filter/pallas_call | solution.py:317
  20.4 1.9 %collective-permute-start.10 = (f32[128,128]{1,0:T(8,128)S(1)}, f32[128,128]{1,0:T(8,128)S(1)}, u32[]{:S(2)}, u32[]{:S(2)}) collective-permute-start(f32[128,128]{1,0:T(8,128)S(1)} %get-tuple-element.26), channel_id=1, source_target_pairs={{0,28},{4,8},{8,4},{12,16},{16,12},{20,24},{24,20},{28,0},{1,29},{... | collective-permute-start | bytes 196616 | tf_op jit(solution)/shard_map/ppermute | solution.py:281
  22.3 0.8 %collective-permute-start.13 = (f32[128,128]{1,0:T(8,128)S(1)}, f32[128,128]{1,0:T(8,128)S(1)}, u32[]{:S(2)}, u32[]{:S(2)}) collective-permute-start(f32[128,128]{1,0:T(8,128)S(1)} %get-tuple-element.29), channel_id=1, source_target_pairs={{0,28},{4,8},{8,4},{12,16},{16,12},{20,24},{24,20},{28,0},{1,29},{... | collective-permute-start | bytes 196616 | tf_op jit(solution)/shard_map/ppermute | solution.py:281
  23.1 0.6 %collective-permute-start.14 = (f32[128,128]{1,0:T(8,128)S(1)}, f32[128,128]{1,0:T(8,128)S(1)}, u32[]{:S(2)}, u32[]{:S(2)}) collective-permute-start(f32[128,128]{1,0:T(8,128)S(1)} %get-tuple-element.30), channel_id=1, source_target_pairs={{0,4},{4,0},{8,12},{12,8},{16,20},{20,16},{24,28},{28,24},{1,5},{5... | collective-permute-start | bytes 196616 | tf_op jit(solution)/shard_map/ppermute | solution.py:282
  23.7 1.8 %collective-permute-start.8 = (f32[128,256]{1,0:T(8,128)S(1)}, f32[128,256]{1,0:T(8,128)S(1)}, u32[]{:S(2)}, u32[]{:S(2)}) collective-permute-start(f32[128,256]{1,0:T(8,128)S(1)} %get-tuple-element.23), channel_id=1, source_target_pairs={{0,28},{4,8},{8,4},{12,16},{16,12},{20,24},{24,20},{28,0},{1,29},{... | collective-permute-start | bytes 393224 | tf_op jit(solution)/shard_map/ppermute | solution.py:281
  25.5 0.2 collective-permute-done.10
  25.7 0.1 collective-permute-start.12
  25.8 1.1 %collective-permute-done.13 = f32[128,128]{1,0:T(8,128)S(1)} collective-permute-done((f32[128,128]{1,0:T(8,128)S(1)}, f32[128,128]{1,0:T(8,128)S(1)}, u32[]{:S(2)}, u32[]{:S(2)}) %collective-permute-start.13) | collective-permute-done | bytes 65568 | tf_op jit(solution)/shard_map/ppermute | solution.py:281
  26.9 2.7 %collective-permute-start.15 = (f32[128,128]{1,0:T(8,128)S(1)}, f32[128,128]{1,0:T(8,128)S(1)}, u32[]{:S(2)}, u32[]{:S(2)}) collective-permute-start(f32[128,128]{1,0:T(8,128)S(1)} %add_add_fusion), channel_id=1, source_target_pairs={{0,3},{1,0},{2,1},{3,2},{4,7},{5,4},{6,5},{7,6},{8,11},{9,8},{10,9... | collective-permute-start | bytes 196616 | tf_op jit(solution)/shard_map/ppermute | solution.py:273
  29.7 2.9 %collective-permute-done.12 = f32[128,128]{1,0:T(8,128)S(1)} collective-permute-done((f32[128,128]{1,0:T(8,128)S(1)}, f32[128,128]{1,0:T(8,128)S(1)}, u32[]{:S(2)}, u32[]{:S(2)}) %collective-permute-start.12) | collective-permute-done | bytes 65568 | tf_op jit(solution)/shard_map/ppermute | solution.py:273
  32.5 0.1 collective-permute-done.15
  32.6 0.7 %maximum_add_fusion = f32[128,256]{1,0:T(8,128)} fusion(f32[128,128]{1,0:T(8,128)S(1)} %collective-permute-done.15, f32[128,128]{1,0:T(8,128)S(1)} %collective-permute-done.12, f32[128,256]{1,0:T(8,128)S(1)} %collective-permute-done.9, f32[128,256]{1,0:T(8,128)S(1)} %get-tuple-element.22, f32[128,256]{1,0:T(8,128)S(1)} %collective-permute-done.8), kind=kLoop, calls=%fused_computation | loop fusion | flops 131072 | bytes 655360 | tf_op jit(solution)/shard_map/add | solution.py:332
  (21 shorter events, 0.1 us)
Async XLA Ops:
  0.9 7.5 %collective-permute-start.2 = (f32[128,128]{1,0:T(8,128)S(1)}, f32[128,128]{1,0:T(8,128)S(1)}, u32[]{:S(2)}, u32[]{:S(2)}) collective-permute-start(f32[128,128]{1,0:T(8,128)S(1)} %get-tuple-element.32), channel_id=1, source_target_pairs={{0,1},{1,2},{2,3},{3,0},{4,5},{5,6},{6,7},{7,4},{8,9},{9,10},{10,1... | collective-permute-start | bytes 196616 | tf_op jit(solution)/shard_map/ppermute | solution.py:273
  4.0 14.1 %copy-start = (bf16[22,256,256]{2,1,0:T(8,128)(2,1)S(1)}, bf16[22,256,256]{2,1,0:T(8,128)(2,1)}, u32[]{:S(2)}) copy-start(bf16[22,256,256]{2,1,0:T(8,128)(2,1)} %constant.2.clone.tables_ref) | copy-start | bytes 8650756
  4.0 14.1 %copy-start.1 = (f32[128,256]{1,0:T(8,128)S(1)}, f32[128,256]{1,0:T(8,128)}, u32[]{:S(2)}) copy-start(f32[128,256]{1,0:T(8,128)} %mid_own.1) | copy-start | bytes 393220
  4.0 7.4 %collective-permute-start.5 = (f32[128,128]{1,0:T(8,128)S(1)}, f32[128,128]{1,0:T(8,128)S(1)}, u32[]{:S(2)}, u32[]{:S(2)}) collective-permute-start(f32[128,128]{1,0:T(8,128)S(1)} %get-tuple-element.31), channel_id=1, source_target_pairs={{0,3},{1,0},{2,1},{3,2},{4,7},{5,4},{6,5},{7,6},{8,11},{9,8},{10,9... | collective-permute-start | bytes 196616 | tf_op jit(solution)/shard_map/ppermute | solution.py:273
  8.4 3.7 %collective-permute-start.4 = (f32[128,128]{1,0:T(8,128)S(1)}, f32[128,128]{1,0:T(8,128)S(1)}, u32[]{:S(2)}, u32[]{:S(2)}) collective-permute-start(f32[128,128]{1,0:T(8,128)S(1)} %collective-permute-done.2.left_own), channel_id=1, source_target_pairs={{0,4},{4,0},{8,12},{12,8},{16,20},{20,16},{24,28},{28,24},{1,5},{5... | collective-permute-start | bytes 196616 | tf_op jit(solution)/shard_map/ppermute | solution.py:282
  8.4 9.7 %collective-permute-start.1 = (f32[128,256]{1,0:T(8,128)}, f32[128,256]{1,0:T(8,128)S(1)}, u32[]{:S(2)}, u32[]{:S(2)}) collective-permute-start(f32[128,256]{1,0:T(8,128)} %mid_own.1), channel_id=1, source_target_pairs={{0,4},{4,0},{8,12},{12,8},{16,20},{20,16},{24,28},{28,24},{1,5},{5... | collective-permute-start | bytes 393224 | tf_op jit(solution)/shard_map/ppermute | solution.py:282
  8.9 9.2 %collective-permute-start = (f32[128,256]{1,0:T(8,128)}, f32[128,256]{1,0:T(8,128)S(1)}, u32[]{:S(2)}, u32[]{:S(2)}) collective-permute-start(f32[128,256]{1,0:T(8,128)} %mid_own.1), channel_id=1, source_target_pairs={{0,28},{4,8},{8,4},{12,16},{16,12},{20,24},{24,20},{28,0},{1,29},{... | collective-permute-start | bytes 393224 | tf_op jit(solution)/shard_map/ppermute | solution.py:281
  11.4 7.2 %collective-permute-start.7 = (f32[128,128]{1,0:T(8,128)S(1)}, f32[128,128]{1,0:T(8,128)S(1)}, u32[]{:S(2)}, u32[]{:S(2)}) collective-permute-start(f32[128,128]{1,0:T(8,128)S(1)} %collective-permute-done.5.right_own), channel_id=1, source_target_pairs={{0,4},{4,0},{8,12},{12,8},{16,20},{20,16},{24,28},{28,24},{1,5},{5... | collective-permute-start | bytes 196616 | tf_op jit(solution)/shard_map/ppermute | solution.py:282
  11.4 7.2 %collective-permute-start.6 = (f32[128,128]{1,0:T(8,128)S(1)}, f32[128,128]{1,0:T(8,128)S(1)}, u32[]{:S(2)}, u32[]{:S(2)}) collective-permute-start(f32[128,128]{1,0:T(8,128)S(1)} %collective-permute-done.5.right_own), channel_id=1, source_target_pairs={{0,28},{4,8},{8,4},{12,16},{16,12},{20,24},{24,20},{28,0},{1,29},{... | collective-permute-start | bytes 196616 | tf_op jit(solution)/shard_map/ppermute | solution.py:281
  12.0 6.0 %collective-permute-start.3 = (f32[128,128]{1,0:T(8,128)S(1)}, f32[128,128]{1,0:T(8,128)S(1)}, u32[]{:S(2)}, u32[]{:S(2)}) collective-permute-start(f32[128,128]{1,0:T(8,128)S(1)} %collective-permute-done.2.left_own), channel_id=1, source_target_pairs={{0,28},{4,8},{8,4},{12,16},{16,12},{20,24},{24,20},{28,0},{1,29},{... | collective-permute-start | bytes 196616 | tf_op jit(solution)/shard_map/ppermute | solution.py:281
  14.0 1.1 %copy-start.2 = (f32[384,512]{1,0:T(8,128)S(1)}, f32[384,512]{1,0:T(8,128)}, u32[]{:S(2)}) copy-start(f32[384,512]{1,0:T(8,128)} %root_ref.1) | copy-start | bytes 2359300
  20.4 5.3 %collective-permute-start.10 = (f32[128,128]{1,0:T(8,128)S(1)}, f32[128,128]{1,0:T(8,128)S(1)}, u32[]{:S(2)}, u32[]{:S(2)}) collective-permute-start(f32[128,128]{1,0:T(8,128)S(1)} %get-tuple-element.26), channel_id=1, source_target_pairs={{0,28},{4,8},{8,4},{12,16},{16,12},{20,24},{24,20},{28,0},{1,29},{... | collective-permute-start | bytes 196616 | tf_op jit(solution)/shard_map/ppermute | solution.py:281
  22.3 3.4 %collective-permute-start.11 = (f32[128,128]{1,0:T(8,128)S(1)}, f32[128,128]{1,0:T(8,128)S(1)}, u32[]{:S(2)}, u32[]{:S(2)}) collective-permute-start(f32[128,128]{1,0:T(8,128)S(1)} %get-tuple-element.27), channel_id=1, source_target_pairs={{0,4},{4,0},{8,12},{12,8},{16,20},{20,16},{24,28},{28,24},{1,5},{5... | collective-permute-start | bytes 196616 | tf_op jit(solution)/shard_map/ppermute | solution.py:282
  22.3 4.6 %collective-permute-start.13 = (f32[128,128]{1,0:T(8,128)S(1)}, f32[128,128]{1,0:T(8,128)S(1)}, u32[]{:S(2)}, u32[]{:S(2)}) collective-permute-start(f32[128,128]{1,0:T(8,128)S(1)} %get-tuple-element.29), channel_id=1, source_target_pairs={{0,28},{4,8},{8,4},{12,16},{16,12},{20,24},{24,20},{28,0},{1,29},{... | collective-permute-start | bytes 196616 | tf_op jit(solution)/shard_map/ppermute | solution.py:281
  23.1 3.8 %collective-permute-start.14 = (f32[128,128]{1,0:T(8,128)S(1)}, f32[128,128]{1,0:T(8,128)S(1)}, u32[]{:S(2)}, u32[]{:S(2)}) collective-permute-start(f32[128,128]{1,0:T(8,128)S(1)} %get-tuple-element.30), channel_id=1, source_target_pairs={{0,4},{4,0},{8,12},{12,8},{16,20},{20,16},{24,28},{28,24},{1,5},{5... | collective-permute-start | bytes 196616 | tf_op jit(solution)/shard_map/ppermute | solution.py:282
  23.7 9.0 %collective-permute-start.8 = (f32[128,256]{1,0:T(8,128)S(1)}, f32[128,256]{1,0:T(8,128)S(1)}, u32[]{:S(2)}, u32[]{:S(2)}) collective-permute-start(f32[128,256]{1,0:T(8,128)S(1)} %get-tuple-element.23), channel_id=1, source_target_pairs={{0,28},{4,8},{8,4},{12,16},{16,12},{20,24},{24,20},{28,0},{1,29},{... | collective-permute-start | bytes 393224 | tf_op jit(solution)/shard_map/ppermute | solution.py:281
  25.7 7.0 %collective-permute-start.9 = (f32[128,256]{1,0:T(8,128)S(1)}, f32[128,256]{1,0:T(8,128)S(1)}, u32[]{:S(2)}, u32[]{:S(2)}) collective-permute-start(f32[128,256]{1,0:T(8,128)S(1)} %get-tuple-element.24), channel_id=1, source_target_pairs={{0,4},{4,0},{8,12},{12,8},{16,20},{20,16},{24,28},{28,24},{1,5},{5... | collective-permute-start | bytes 393224 | tf_op jit(solution)/shard_map/ppermute | solution.py:282
  25.7 6.8 %collective-permute-start.12 = (f32[128,128]{1,0:T(8,128)S(1)}, f32[128,128]{1,0:T(8,128)S(1)}, u32[]{:S(2)}, u32[]{:S(2)}) collective-permute-start(f32[128,128]{1,0:T(8,128)S(1)} %add_add_fusion.1), channel_id=1, source_target_pairs={{0,1},{1,2},{2,3},{3,0},{4,5},{5,6},{6,7},{7,4},{8,9},{9,10},{10,1... | collective-permute-start | bytes 196616 | tf_op jit(solution)/shard_map/ppermute | solution.py:273
  26.9 5.7 %collective-permute-start.15 = (f32[128,128]{1,0:T(8,128)S(1)}, f32[128,128]{1,0:T(8,128)S(1)}, u32[]{:S(2)}, u32[]{:S(2)}) collective-permute-start(f32[128,128]{1,0:T(8,128)S(1)} %add_add_fusion), channel_id=1, source_target_pairs={{0,3},{1,0},{2,1},{3,2},{4,7},{5,4},{6,5},{7,6},{8,11},{9,8},{10,9... | collective-permute-start | bytes 196616 | tf_op jit(solution)/shard_map/ppermute | solution.py:273
